TPU v7x, 32 devices: a whole 2x2x4 slice. The times are simulated.
32 devices in a mesh: parts: 2 (over x), inner: 16 (over z, y, core).
Axes of the slice: x: 2, y: 2, z: 4, core: 2. Of those that a mesh axis runs over, the one named last changes fastest.
Arguments:
- stem_slab: bfloat16 [2, 16384, 1024], P(None, ('parts', 'inner')), parts along dimension 1, may hold values from -6 to 6
- branches: bfloat16 [3, 2, 1024, 1024], P(None, None, 'inner'), may hold values from -0.1875 to 0.1875
- column_order: int32 [3, 1024], replicated, may hold values from 0 to 1023, each once within a row
Outputs:
- result_slab: bfloat16 [2, 16384, 1024], P(None, ('parts', 'inner')), parts along dimension 1
There are 2 independent parts, one for each index of `parts`. A program takes and returns all parts, laid end to end along the dimension named above; an argument that names none is the same for every part. Nothing has to cross between parts.
Inputs may be any that keep to these rules, and one draw needn't show every extreme that they name: Each row of column_order names every number from 0 to 1023 exactly once.
All inputs are finite; a program needn't handle non-finite values.
Results may differ from a plain program's by a relative error of at most 0.0057.
Values may be sent and summed in bfloat16 or wider, within the bound.
No kernel may reach another device: no remote copies, remote signals or barrier semaphores. Data moves between devices by JAX's collectives and lax.ppermute only.
A program may use at most 64 MiB of HBM per device.

v0:
```python
import jax
import jax.numpy as jnp
from jax import lax
from jax.sharding import PartitionSpec as P

STEPS = 3


def add_block(ordered, block_rows):
    real_part = jnp.dot(ordered[0], block_rows[0], preferred_element_type=jnp.float32) - jnp.dot(
        ordered[1], block_rows[1], preferred_element_type=jnp.float32
    )
    imag_part = jnp.dot(ordered[0], block_rows[1], preferred_element_type=jnp.float32) + jnp.dot(
        ordered[1], block_rows[0], preferred_element_type=jnp.float32
    )
    return jnp.stack([real_part, imag_part])


def folded(slab, order_row, branch_slice):
    ordered = jnp.take(slab, order_row, axis=2)
    summed = add_block(ordered, lax.all_gather(branch_slice, "inner", axis=1, tiled=True))
    return summed.astype(jnp.bfloat16)


def local(stem_slab, branches, column_order):
    current = folded(stem_slab, column_order[0], branches[0])
    for section_index in range(1, STEPS):
        current = lax.all_to_all(current, "inner", split_axis=2, concat_axis=2, tiled=True)
        current = folded(current, column_order[section_index], branches[section_index])
    return current


def solution(mesh):
    in_specs = (P(None, ("parts", "inner"), None), P(None, None, "inner", None), P())
    out_specs = P(None, ("parts", "inner"), None)
    return jax.shard_map(local, mesh=mesh, in_specs=in_specs, out_specs=out_specs, check_vma=False)
```

profile of v0, /device:TPU:13, one launch (start us, length us, event | category | flops | bytes accessed | tf_op | source)
XLA Modules:
  0.0 274.1 jit_solution(2985922748747807240)
XLA Ops:
  6.5 0.0 copy-start
  6.5 0.0 all-gather.7.cloned.1.call-start
  6.5 2.2 fusion.39
  8.7 0.0 all-gather.7.cloned.1.call-update
  8.8 0.0 all-gather.9.cloned.1.call-start
  8.8 0.7 all-gather.9.cloned.1.call-update
  9.5 0.0 copy-done
  9.5 0.0 copy-start.4
  9.5 4.0 %copy.16 = bf16[2,512,1024]{1,0,2:T(2,128)(2,1)} copy(bf16[2,512,1024]{2,1,0:T(8,128)(2,1)S(1)} %copy-done) | data formatting | bytes 4194304 | tf_op args[0]
  13.6 0.0 copy-done.4
  13.6 7.5 %gather_fusion = bf16[1024,2,512]{2,1,0:T(2,128)(2,1)S(1)} fusion(bf16[2,512,1024]{1,0,2:T(2,128)(2,1)} %copy.16, s32[1024]{0:T(1024)S(1)} %fusion.33), kind=kCustom, calls=%fused_computation.clone | custom fusion | bytes 4198400 | tf_op jit(solution)/shard_map/jit(_take)/gather | solution.py:20
  21.1 3.9 %fusion = bf16[2,512,1024]{1,0,2:T(2,128)(2,1)S(1)} fusion(bf16[1024,2,512]{2,1,0:T(2,128)(2,1)S(1)} %gather_fusion, pred[1024]{0:T(1024)(128)(4,1)S(1)} %compare_and_fusion.2), kind=kLoop, calls=%fused_computation.21 | loop fusion | flops 1048576 | bytes 4195328 | tf_op jit(solution)/shard_map/jit(_take)/select_n | solution.py:20
  25.0 3.8 %fusion.38 = (bf16[1,512,1024]{1,0,2:T(2,128)(2,1)}, bf16[1,512,1024]{1,0,2:T(2,128)(2,1)S(1)}) fusion(bf16[2,512,1024]{1,0,2:T(2,128)(2,1)S(1)} %fusion), kind=kLoop, calls=%fused_computation.65 | loop fusion | bytes 4194304 | tf_op jit(solution)/shard_map/slice | solution.py:10
  28.8 4.6 %copy.17 = bf16[1,512,1024]{2,1,0:T(8,128)(2,1)S(1)} copy(bf16[1,512,1024]{1,0,2:T(2,128)(2,1)} %get-tuple-element.10) | data formatting | bytes 2097152 | tf_op jit(solution)/shard_map/slice | solution.py:10
  33.4 4.2 %copy.18 = bf16[1,512,1024]{2,1,0:T(8,128)(2,1)} copy(bf16[1,512,1024]{1,0,2:T(2,128)(2,1)S(1)} %get-tuple-element.11) | data formatting | bytes 2097152 | tf_op jit(solution)/shard_map/slice | solution.py:11
  37.6 0.0 copy-start.1
  37.6 23.0 %all-gather.7.cloned.1.call-done = bf16[1,2,1024,1024]{3,2,1,0:T(8,128)(2,1)} async-done(((bf16[1,2,64,1024]{3,2,1,0:T(8,128)(2,1)}), bf16[1,2,1024,1024]{3,2,1,0:T(8,128)(2,1)}) %all-gather.7.cloned.1.call-update) | async-done | bytes 4194320 | tf_op jit(solution)/shard_map/all_gather | solution.py:21
  60.6 0.0 copy-start.7
  60.6 3.0 %fusion.4 = f32[512,1024]{1,0:T(8,128)S(1)} fusion(bf16[1,2,1024,1024]{3,2,1,0:T(8,128)(2,1)} %all-gather.7.cloned.1.call-done, bf16[1,512,1024]{2,1,0:T(8,128)(2,1)S(1)} %copy.17), kind=kOutput, calls=%fused_computation.25 | convolution fusion | flops 1073741824 | bytes 5242880 | tf_op jit(solution)/shard_map/dot_general | solution.py:10
  63.6 0.0 copy-done.1
  63.6 0.0 copy-done.7
  63.6 1.3 fusion.3
  64.9 1.3 fusion.15
  66.2 1.3 fusion.16
  67.5 0.2 pad_maximum_fusion
  67.7 4.0 %copy.19 = bf16[2,512,1024]{1,0,2:T(2,128)(2,1)} copy(bf16[2,512,1024]{2,1,0:T(8,128)(2,1)S(1)} %pad_maximum_fusion) | data formatting | bytes 4194304 | tf_op jit(solution)/shard_map/stack | solution.py:16
  71.7 5.5 %all-to-all-start = ((bf16[2,512,1024]{1,0,2:T(2,128)(2,1)}), bf16[2,512,1024]{1,0,2:T(2,128)(2,1)}, u32[]{:S(2)}, u32[]{:S(2)}) async-start(bf16[2,512,1024]{1,0,2:T(2,128)(2,1)} %copy.19), calls=%async_computation | async-start | bytes 4194304 | tf_op jit(solution)/shard_map/all_to_all | solution.py:28
  77.2 0.2 all-gather.11.cloned.1.call-start
  77.4 0.5 all-gather.11.cloned.1.call-update
  78.0 66.4 %all-to-all-done = bf16[2,512,1024]{1,0,2:T(2,128)(2,1)} async-done(((bf16[2,512,1024]{1,0,2:T(2,128)(2,1)}), bf16[2,512,1024]{1,0,2:T(2,128)(2,1)}, u32[]{:S(2)}, u32[]{:S(2)}) %all-to-all-start) | async-done | bytes 2097184 | tf_op jit(solution)/shard_map/all_to_all | solution.py:28
  144.3 7.5 %gather_fusion.1 = bf16[1024,2,512]{2,1,0:T(2,128)(2,1)S(1)} fusion(bf16[2,512,1024]{1,0,2:T(2,128)(2,1)} %all-to-all-done, s32[1024]{0:T(1024)S(1)} %fusion.34), kind=kCustom, calls=%fused_computation.1.clone | custom fusion | bytes 4198400 | tf_op jit(solution)/shard_map/jit(_take)/gather | solution.py:20
  151.8 3.9 %fusion.1 = bf16[2,512,1024]{1,0,2:T(2,128)(2,1)S(1)} fusion(bf16[1024,2,512]{2,1,0:T(2,128)(2,1)S(1)} %gather_fusion.1, pred[1024]{0:T(1024)(128)(4,1)S(1)} %compare_and_fusion.1), kind=kLoop, calls=%fused_computation.22 | loop fusion | flops 1048576 | bytes 4195328 | tf_op jit(solution)/shard_map/jit(_take)/select_n | solution.py:20
  155.7 3.8 %fusion.37 = (bf16[1,512,1024]{1,0,2:T(2,128)(2,1)}, bf16[1,512,1024]{1,0,2:T(2,128)(2,1)S(1)}) fusion(bf16[2,512,1024]{1,0,2:T(2,128)(2,1)S(1)} %fusion.1), kind=kLoop, calls=%fused_computation.64 | loop fusion | bytes 4194304 | tf_op jit(solution)/shard_map/slice | solution.py:10
  159.5 4.6 %copy.20 = bf16[1,512,1024]{2,1,0:T(8,128)(2,1)S(1)} copy(bf16[1,512,1024]{1,0,2:T(2,128)(2,1)} %get-tuple-element.8) | data formatting | bytes 2097152 | tf_op jit(solution)/shard_map/slice | solution.py:10
  164.1 4.2 %copy.21 = bf16[1,512,1024]{2,1,0:T(8,128)(2,1)} copy(bf16[1,512,1024]{1,0,2:T(2,128)(2,1)S(1)} %get-tuple-element.9) | data formatting | bytes 2097152 | tf_op jit(solution)/shard_map/slice | solution.py:11
  168.3 0.0 copy-start.2
  168.3 0.0 all-gather.9.cloned.1.call-done
  168.3 0.0 copy-start.5
  168.3 3.4 %fusion.8 = f32[512,1024]{1,0:T(8,128)S(1)} fusion(bf16[1,2,1024,1024]{3,2,1,0:T(8,128)(2,1)} %all-gather.9.cloned.1.call-done, bf16[1,512,1024]{2,1,0:T(8,128)(2,1)S(1)} %copy.20), kind=kOutput, calls=%fused_computation.29 | convolution fusion | flops 1073741824 | bytes 5242880 | tf_op jit(solution)/shard_map/dot_general | solution.py:10
  171.7 0.0 copy-done.2
  171.8 0.2 copy-done.5
  171.9 1.3 fusion.7
  173.2 1.3 fusion.17
  174.5 1.3 fusion.18
  175.8 0.2 pad_maximum_fusion.1
  176.0 4.0 %copy.22 = bf16[2,512,1024]{1,0,2:T(2,128)(2,1)} copy(bf16[2,512,1024]{2,1,0:T(8,128)(2,1)S(1)} %pad_maximum_fusion.1) | data formatting | bytes 4194304 | tf_op jit(solution)/shard_map/stack | solution.py:16
  180.0 5.0 %all-to-all-start.1 = ((bf16[2,512,1024]{1,0,2:T(2,128)(2,1)}), bf16[2,512,1024]{1,0,2:T(2,128)(2,1)}, u32[]{:S(2)}, u32[]{:S(2)}) async-start(bf16[2,512,1024]{1,0,2:T(2,128)(2,1)} %copy.22), calls=%async_computation.1 | async-start | bytes 4194304 | tf_op jit(solution)/shard_map/all_to_all | solution.py:28
  185.1 50.1 %all-to-all-done.1 = bf16[2,512,1024]{1,0,2:T(2,128)(2,1)} async-done(((bf16[2,512,1024]{1,0,2:T(2,128)(2,1)}), bf16[2,512,1024]{1,0,2:T(2,128)(2,1)}, u32[]{:S(2)}, u32[]{:S(2)}) %all-to-all-start.1) | async-done | bytes 2097184 | tf_op jit(solution)/shard_map/all_to_all | solution.py:28
  235.1 7.5 %gather_fusion.2 = bf16[1024,2,512]{2,1,0:T(2,128)(2,1)S(1)} fusion(bf16[2,512,1024]{1,0,2:T(2,128)(2,1)} %all-to-all-done.1, s32[1024]{0:T(1024)S(1)} %fusion.35), kind=kCustom, calls=%fused_computation.2.clone | custom fusion | bytes 4198400 | tf_op jit(solution)/shard_map/jit(_take)/gather | solution.py:20
  242.6 3.9 %fusion.2 = bf16[2,512,1024]{1,0,2:T(2,128)(2,1)S(1)} fusion(bf16[1024,2,512]{2,1,0:T(2,128)(2,1)S(1)} %gather_fusion.2, pred[1024]{0:T(1024)(128)(4,1)S(1)} %compare_and_fusion), kind=kLoop, calls=%fused_computation.23 | loop fusion | flops 1048576 | bytes 4195328 | tf_op jit(solution)/shard_map/jit(_take)/select_n | solution.py:20
  246.5 3.8 %fusion.36 = (bf16[1,512,1024]{1,0,2:T(2,128)(2,1)}, bf16[1,512,1024]{1,0,2:T(2,128)(2,1)S(1)}) fusion(bf16[2,512,1024]{1,0,2:T(2,128)(2,1)S(1)} %fusion.2), kind=kLoop, calls=%fused_computation.63 | loop fusion | bytes 4194304 | tf_op jit(solution)/shard_map/slice | solution.py:10
  250.3 4.6 %copy.23 = bf16[1,512,1024]{2,1,0:T(8,128)(2,1)S(1)} copy(bf16[1,512,1024]{1,0,2:T(2,128)(2,1)} %get-tuple-element.6) | data formatting | bytes 2097152 | tf_op jit(solution)/shard_map/slice | solution.py:10
  254.9 4.2 %copy.24 = bf16[1,512,1024]{2,1,0:T(8,128)(2,1)} copy(bf16[1,512,1024]{1,0,2:T(2,128)(2,1)S(1)} %get-tuple-element.7) | data formatting | bytes 2097152 | tf_op jit(solution)/shard_map/slice | solution.py:11
  259.1 0.0 copy-start.3
  259.1 0.0 all-gather.11.cloned.1.call-done
  259.1 0.0 copy-start.6
  259.1 3.0 %fusion.12 = f32[512,1024]{1,0:T(8,128)S(1)} fusion(bf16[1,2,1024,1024]{3,2,1,0:T(8,128)(2,1)} %all-gather.11.cloned.1.call-done, bf16[1,512,1024]{2,1,0:T(8,128)(2,1)S(1)} %copy.23), kind=kOutput, calls=%fused_computation.33 | convolution fusion | flops 1073741824 | bytes 5242880 | tf_op jit(solution)/shard_map/dot_general | solution.py:10
  262.1 0.0 copy-done.3
  262.1 0.1 copy-done.6
  262.3 1.3 fusion.11
  263.5 1.3 fusion.19
  264.8 1.3 fusion.20
  266.1 1.5 pad_maximum_fusion.2
  (7 shorter events, 0.1 us)
Async XLA Ops:
  6.5 3.0 %copy-start = (bf16[2,512,1024]{2,1,0:T(8,128)(2,1)S(1)}, bf16[2,512,1024]{2,1,0:T(8,128)(2,1)}, u32[]{:S(2)}) copy-start(bf16[2,512,1024]{2,1,0:T(8,128)(2,1)} %param.5) | copy-start | bytes 6291460
  6.5 54.1 %all-gather.7.cloned.1.call-start = ((), (), s32[]{:S(2)}) async-start(), calls=%async_computation.2 | async-start | bytes 4456448 | tf_op jit(solution)/shard_map/all_gather | solution.py:21
  8.8 159.5 %all-gather.9.cloned.1.call-start = ((), (), s32[]{:S(2)}) async-start(), calls=%async_computation.3 | async-start | bytes 4456448 | tf_op jit(solution)/shard_map/all_gather | solution.py:21
  9.5 4.1 %copy-start.4 = (s32[3,1024]{1,0:T(4,128)S(1)}, s32[3,1024]{1,0:T(4,128)}, u32[]{:S(2)}) copy-start(s32[3,1024]{1,0:T(4,128)} %param.7) | copy-start | bytes 36868
  37.6 26.0 %copy-start.1 = (bf16[1,512,1024]{2,1,0:T(8,128)(2,1)S(1)}, bf16[1,512,1024]{2,1,0:T(8,128)(2,1)}, u32[]{:S(2)}) copy-start(bf16[1,512,1024]{2,1,0:T(8,128)(2,1)} %copy.18) | copy-start | bytes 3145732
  60.6 3.0 %copy-start.7 = (bf16[1,2,1024,1024]{3,2,1,0:T(8,128)(2,1)S(1)}, bf16[1,2,1024,1024]{3,2,1,0:T(8,128)(2,1)}, u32[]{:S(2)}) copy-start(bf16[1,2,1024,1024]{3,2,1,0:T(8,128)(2,1)} %all-gather.7.cloned.1.call-done) | copy-start | bytes 12582916
  71.7 72.6 %all-to-all-start = ((bf16[2,512,1024]{1,0,2:T(2,128)(2,1)}), bf16[2,512,1024]{1,0,2:T(2,128)(2,1)}, u32[]{:S(2)}, u32[]{:S(2)}) async-start(bf16[2,512,1024]{1,0,2:T(2,128)(2,1)} %copy.19), calls=%async_computation | async-start | bytes 4194304 | tf_op jit(solution)/shard_map/all_to_all | solution.py:28
  77.2 181.9 %all-gather.11.cloned.1.call-start = ((), (), s32[]{:S(2)}) async-start(), calls=%async_computation.4 | async-start | bytes 4456448 | tf_op jit(solution)/shard_map/all_gather | solution.py:21
  168.3 3.4 %copy-start.2 = (bf16[1,512,1024]{2,1,0:T(8,128)(2,1)S(1)}, bf16[1,512,1024]{2,1,0:T(8,128)(2,1)}, u32[]{:S(2)}) copy-start(bf16[1,512,1024]{2,1,0:T(8,128)(2,1)} %copy.21) | copy-start | bytes 3145732
  168.3 3.6 %copy-start.5 = (bf16[1,2,1024,1024]{3,2,1,0:T(8,128)(2,1)S(1)}, bf16[1,2,1024,1024]{3,2,1,0:T(8,128)(2,1)}, u32[]{:S(2)}) copy-start(bf16[1,2,1024,1024]{3,2,1,0:T(8,128)(2,1)} %all-gather.9.cloned.1.call-done) | copy-start | bytes 12582916
  180.0 55.1 %all-to-all-start.1 = ((bf16[2,512,1024]{1,0,2:T(2,128)(2,1)}), bf16[2,512,1024]{1,0,2:T(2,128)(2,1)}, u32[]{:S(2)}, u32[]{:S(2)}) async-start(bf16[2,512,1024]{1,0,2:T(2,128)(2,1)} %copy.22), calls=%async_computation.1 | async-start | bytes 4194304 | tf_op jit(solution)/shard_map/all_to_all | solution.py:28
  259.1 3.0 %copy-start.3 = (bf16[1,512,1024]{2,1,0:T(8,128)(2,1)S(1)}, bf16[1,512,1024]{2,1,0:T(8,128)(2,1)}, u32[]{:S(2)}) copy-start(bf16[1,512,1024]{2,1,0:T(8,128)(2,1)} %copy.24) | copy-start | bytes 3145732
  259.1 3.1 %copy-start.6 = (bf16[1,2,1024,1024]{3,2,1,0:T(8,128)(2,1)S(1)}, bf16[1,2,1024,1024]{3,2,1,0:T(8,128)(2,1)}, u32[]{:S(2)}) copy-start(bf16[1,2,1024,1024]{3,2,1,0:T(8,128)(2,1)} %all-gather.11.cloned.1.call-done) | copy-start | bytes 12582916
Sparse Core Ops, SparseCore 0:
  9.5 51.0 all-gather.6
  62.8 73.3 all-gather.8
  138.4 54.5 all-gather.10
where the time goes:
time: 275 us; the launch traced here: 274 us
  waiting for transfers between devices  141 us (51%)
  local copies, waits for them, and re-layouts  74.9 us (27%)
  matrix products  20.8 us (8%)
  other arithmetic  13.7 us (5%)
  between operations  13.4 us (5%)
  starting transfers between devices  10.8 us (4%)
    all_to_all x2, waiting for transfers between devices, local(): lax.all_to_all(current, 'inner', split_axis=2, concat_axis=2, tiled=True)  116 us
    slice x6, local copies, waits for them, and re-layouts, add_block(): ordered[0]  25.1 us
    all_gather x3, waiting for transfers between devices, folded(): lax.all_gather(branch_slice, 'inner', axis=1, tiled=True)  23 us
    gather x3, local copies, waits for them, and re-layouts, folded(): ordered = jnp.take(slab, order_row, axis=2)  22.4 us
    slice x3, local copies, waits for them, and re-layouts, add_block(): ordered[1]  12.7 us
    select_n x3, other arithmetic, folded(): ordered = jnp.take(slab, order_row, axis=2)  11.8 us
    all_to_all x2, starting transfers between devices, local(): lax.all_to_all(current, 'inner', split_axis=2, concat_axis=2, tiled=True)  10.5 us
    dot_general x3, matrix products, add_block(): jnp.dot(ordered[0], block_rows[0], preferred_element_type=jnp.float32)  9.41 us
  transfers between devices with their start and end apart: 5, of which 3 were waited for; matrix products, arithmetic and copies ran while one was open for 36% of the time, Pallas kernels for 0%

commit v1 on v0

v1 whole, which is shorter than its diff:
```python
import functools

import jax
import jax.numpy as jnp
from jax import lax
from jax.experimental import pallas as pl
from jax.experimental.pallas import tpu as pltpu
from jax.sharding import PartitionSpec as P


LANES = 128
CHUNKS = 2
F32 = jnp.float32
BF16 = jnp.bfloat16
ANY = pl.BlockSpec(memory_space=pltpu.HBM)
VMEM = pl.BlockSpec(memory_space=pltpu.VMEM)
ROOM = pltpu.CompilerParams(vmem_limit_bytes=24 * 1024 * 1024)


def add_block(ordered, block_rows):
    real_part = jnp.dot(ordered[0], block_rows[0], preferred_element_type=F32) - jnp.dot(
        ordered[1], block_rows[1], preferred_element_type=F32
    )
    imag_part = jnp.dot(ordered[0], block_rows[1], preferred_element_type=F32) + jnp.dot(
        ordered[1], block_rows[0], preferred_element_type=F32
    )
    return jnp.stack([real_part, imag_part])


def folded(slab, order_row, branch_slice):
    ordered = jnp.take(slab, order_row, axis=2)
    summed = add_block(ordered, lax.all_gather(branch_slice, "inner", axis=1, tiled=True))
    return summed.astype(BF16)


def plain(stem_slab, branches, column_order):
    current = folded(stem_slab, column_order[0], branches[0])
    for section_index in range(1, branches.shape[0]):
        current = lax.all_to_all(current, "inner", split_axis=2, concat_axis=2, tiled=True)
        current = folded(current, column_order[section_index], branches[section_index])
    return current


def wait_all(ref, sem):
    pltpu.make_async_copy(ref, ref, sem).wait()


def branch_tile(places, refs, section, mine, columns):
    rows = {}
    for at, item, half, j, first in places:
        ref = refs[at] if item is None else refs[at].at[item]
        if half is None:
            rows[0, j] = ref[first + section, mine, :, columns]
            rows[1, j] = ref[first + section, 1 - mine, :, columns]
        else:
            rows[half, j] = ref[section, :, columns]
    return [jnp.concatenate([rows[half, j] for j in range(len(rows) // 2)], axis=0) for half in (0, 1)]


def product_tile(x_ref, w_real, w_imag):
    m = x_ref.shape[0] // 2
    by_real = jnp.dot(x_ref[...], w_real, preferred_element_type=F32)
    by_imag = jnp.dot(x_ref[...], w_imag, preferred_element_type=F32)
    return by_real[:m] - by_imag[m:], by_imag[:m] + by_real[m:]


def product_tile_halves(x_ref, w_mine, w_other, mine):
    m = x_ref.shape[0] // 2
    by_mine = jnp.dot(x_ref[...], w_mine, preferred_element_type=F32)
    by_other = jnp.dot(x_ref[...], w_other, preferred_element_type=F32)
    by_real = jnp.where(mine == 0, by_mine, by_other)
    by_imag = jnp.where(mine == 0, by_other, by_mine)
    return by_real[:m] - by_imag[m:], by_imag[:m] + by_real[m:]


def reorder(x_in, pick_ref, x_now):
    rows, k = x_now.shape
    x = x_in[...].reshape(rows, k)
    for lo in range(0, k, 2 * LANES):
        columns = pl.ds(lo, 2 * LANES)
        x_now[:, columns] = jnp.dot(x, pick_ref[:, columns], preferred_element_type=F32).astype(BF16)


def mid_kernel(n, q, rc, chunk, places, n_w, scalars, picks, *rest):
    pieces, rest = rest[: n // 2], rest[n // 2 :]
    w_refs, rest = rest[:n_w], rest[n_w:]
    outs, rest = rest[: n // 2], rest[n // 2 :]
    x_in, x_now, y_out = rest
    me, mine = scalars[0], scalars[1]
    for kc, piece in enumerate(pieces):
        x_in[:, 2 * kc : 2 * kc + 2] = piece[:, :, chunk * rc : (chunk + 1) * rc, :]
    k = x_now.shape[1]
    low_half = lax.broadcasted_iota(jnp.int32, (rc, LANES), 1) < q
    tile = 2 * LANES

    def swapped(section, store):
        for lo in range(0, k, tile):
            halves = branch_tile(places, w_refs, section, mine, pl.ds(lo, tile))
            for p, y in enumerate(product_tile_halves(x_now, *halves, mine)):
                for s in range(0, tile, LANES):
                    part = y[:, s : s + LANES]
                    turned = pltpu.roll(part, q, 1)
                    d = (lo + s) // q
                    for j in range(0, n, 2):
                        even, odd = slice(j * rc, (j + 1) * rc), slice((j + 1) * rc, (j + 2) * rc)
                        store(p, d, j * q, jnp.where(low_half, part[even], turned[odd]).astype(BF16))
                        store(p, d + 1, j * q, jnp.where(low_half, turned[even], part[odd]).astype(BF16))

    reorder(x_in, picks.at[0], x_now)

    def store_mid(p, d, lo, value):
        x_in[p, d, :, lo : lo + LANES] = value

    swapped(0, store_mid)
    reorder(x_in, picks.at[1], x_now)

    def store_out(p, h, lo, value):
        y_out[h, p, :, lo : lo + LANES] = value

    swapped(1, store_out)
    for kc in range(n // 2):
        for cr in range(2):
            outs[kc][cr] = y_out[me ^ (2 * kc + cr)]


def join_kernel(items, *refs):
    parts, (out, held, sems) = refs[:-3], refs[-3:]
    for at, (part, item) in enumerate(items):
        source = parts[part] if item is None else parts[part].at[item]
        pltpu.make_async_copy(source, held.at[at], sems.at[0]).start()
    wait_all(held, sems.at[0])
    put = pltpu.make_async_copy(held, out, sems.at[1])
    put.start()
    put.wait()


def turn_kernel(places, n_w, scalars, picks, *rest):
    w_refs, out = rest[:n_w], rest[n_w]
    mine = scalars[1]
    pick = picks[picks.shape[0] - 1]
    for lo in range(0, out.shape[2], 2 * LANES):
        columns = pl.ds(lo, 2 * LANES)
        for half, w in enumerate(branch_tile(places, w_refs, 0, mine, columns)):
            turned = jnp.dot(pick, w, preferred_element_type=F32).astype(BF16)
            out[mine if half == 0 else 1 - mine, :, columns] = turned


def fin_kernel(n, rc, chunk, with_prev, scalars, branch, *rest):
    pieces, forwarded, rest = rest[: n // 2], rest[n // 2], rest[n // 2 + 1 :]
    if with_prev:
        rest = rest[1:]
    out, x_in, y_out, sems = rest
    me = scalars[0]
    for kc, piece in enumerate(pieces):
        x_in[:, 2 * kc] = piece[0]
        x_in[:, 2 * kc + 1] = forwarded[kc]
    k = x_in.shape[3]
    rows = rc * CHUNKS
    tile = 2 * LANES
    x_now = x_in.reshape(2 * n * rc, k)
    for lo in range(0, k, tile):
        for p, y in enumerate(product_tile(x_now, branch[0, :, lo : lo + tile], branch[1, :, lo : lo + tile])):
            y_out[p, :, :, lo : lo + tile] = y.astype(BF16).reshape(n, rc, tile)
    for j in range(n):
        start = pl.multiple_of((me ^ j) * rows + chunk * rc, rc)
        pltpu.make_async_copy(y_out.at[:, j], out.at[:, pl.ds(start, rc)], sems.at[2]).start()
    wait_all(y_out, sems.at[2])


def pick_kernel(q, scalars, order, out, row):
    me, (sections, rows, k) = scalars[0], out.shape
    step = 2 * LANES
    for section in range(sections):
        for at in range(k // LANES):
            block = order[section, pl.ds(at ^ (me >> 1), 1), :]
            row[:, at * LANES : (at + 1) * LANES] = jnp.where((me & 1) == 1, pltpu.roll(block, q, 1), block)
        shift = me * q if section == 1 else 0
        for lo in range(0, rows, step):
            number = lo + lax.broadcasted_iota(jnp.int32, (step, k), 0)
            out[section, lo : lo + step] = ((number ^ shift) == row[...]).astype(F32).astype(BF16)


def prep_kernel(scalars, stem, sib, x, sem):
    core = scalars[0] & 1
    for copy in (
        pltpu.make_async_copy(stem.at[:, :, 1 - core], x, sem),
        pltpu.make_async_copy(x, sib, sem),
    ):
        copy.start()
        copy.wait()


def pack_kernel(scalars, stem, sib, *rest):
    outs, (x, sems) = rest[:-2], rest[-2:]
    core, chip = scalars[0] & 1, scalars[0] >> 1
    takes = [
        pltpu.make_async_copy(stem.at[:, :, core], x.at[0], sems.at[0]),
        pltpu.make_async_copy(sib, x.at[1], sems.at[1]),
    ]
    for take in takes:
        take.start()
    for take in takes:
        take.wait()
    for kc in reversed(range(len(outs))):
        for cr in range(2):
            pltpu.make_async_copy(x.at[cr, :, chip ^ kc], outs[kc].at[:, cr], sems.at[2]).start()
    wait_all(x, sems.at[2])


def forward_kernel(*refs):
    pieces, (out, blocks, sems) = refs[:-3], refs[-3:]
    for kc, piece in enumerate(pieces):
        pltpu.make_async_copy(piece.at[1], blocks.at[kc], sems.at[0]).start()
    wait_all(blocks, sems.at[0])
    put = pltpu.make_async_copy(blocks, out, sems.at[1])
    put.start()
    put.wait()


def flat_cost(flops, size):
    return pl.CostEstimate(flops=flops, bytes_accessed=size, transcendentals=0)


def local(n, stem_slab, branches, column_order):
    chips = n // 2
    rows, k = stem_slab.shape[1:]
    q = k // n
    block = rows // n
    rc = block // CHUNKS
    m = n * rc
    me = lax.axis_index("inner")
    n_parts = lax.axis_size("parts")
    mine_index = lax.axis_index("parts") & 1
    scalars = jnp.stack([me, mine_index]).astype(jnp.int32)

    def swap_inner(x, mask):
        return lax.ppermute(x, "inner", [(i, i ^ mask) for i in range(n)])

    def swap_parts(x):
        return lax.ppermute(x, "parts", [(i, i ^ 1) for i in range(n_parts)])

    smem = pl.BlockSpec(memory_space=pltpu.SMEM)
    vmem = pltpu.VMEM
    sections = column_order.shape[0]
    split = sections - 1
    by_core = stem_slab.reshape(2, chips, 2, block, k)

    def shape(*dims):
        return jax.ShapeDtypeStruct(dims, BF16)

    for_sib = pl.pallas_call(
        prep_kernel,
        out_shape=shape(2, chips, block, k),
        in_specs=[smem, ANY],
        out_specs=ANY,
        scratch_shapes=[vmem((2, chips, block, k), BF16), pltpu.SemaphoreType.DMA],
        cost_estimate=flat_cost(0, 4 * rows * k),
        compiler_params=ROOM,
        name="prep",
    )(scalars, by_core)

    def joined(parts):
        arrays, items = [], []
        for array, item in parts:
            at = next((i for i, other in enumerate(arrays) if other is array), len(arrays))
            arrays[at:] = [array] if at == len(arrays) else arrays[at:]
            items.append((at, item))
        piece = parts[0][0].shape if parts[0][1] is None else parts[0][0].shape[1:]
        whole = shape(len(parts), *piece)
        return pl.pallas_call(
            functools.partial(join_kernel, tuple(items)),
            out_shape=whole,
            in_specs=[ANY] * len(arrays),
            out_specs=ANY,
            scratch_shapes=[vmem(whole.shape, BF16), pltpu.SemaphoreType.DMA((2,))],
            cost_estimate=flat_cost(0, 4 * whole.size),
            compiler_params=ROOM,
        )(*arrays)

    top, low = n // 2, n // 4
    own_sib = swap_inner(branches, 1)

    def start_gather(first, count):
        mine = lax.dynamic_slice(branches, (first, mine_index, 0, 0), (count, 1, q, k))[:, 0]
        far = swap_inner(mine, top | low)
        near = swap_inner(mine, low)
        held = {0: (mine, None), low: (near, None), top | low: (far, None)}
        held[top] = (swap_inner(far, low), None)
        return held

    def finish_gather(held, others, groups, first):
        sources, places = [], []

        def place(value, j, half):
            array, item = value
            at = next((i for i, other in enumerate(sources) if other is array), len(sources))
            sources[at:] = [array] if at == len(sources) else sources[at:]
            places.append((at, item, half, j))

        for group in groups:
            parts = [(held[i], 0, i) for i in group] + [(others[i], 1, i) for i in group]
            got = swap_inner(joined([part[0] for part in parts]), 1)
            for at, (value, half, i) in enumerate(parts):
                place(value, i, half)
                place((got, at), i + 1, half)
        places += [(len(sources), None, None, 0), (len(sources) + 1, None, None, 1)]
        sources += [branches, own_sib]
        shifted = [(at, item, half, j, first if half is None else 0) for at, item, half, j in places]
        return sources, tuple(shifted)

    def gather_by_piece(first, count):
        held = start_gather(first, count)
        bit = low // 2
        while bit >= 2:
            for i in list(held):
                held[i | bit] = (swap_inner(held[i][0], bit), None)
            bit //= 2
        others = {i: (swap_parts(held[i][0]), None) for i in held if i}
        last = [i for i in held if i & 2 and i & top]
        early = [i for i in held if i and i not in last]
        return finish_gather(held, others, [early, last], first)

    def gather_joined(first, count):
        held = start_gather(first, count)
        bit = low // 2
        while bit >= 2:
            now = list(held)
            got = swap_inner(joined([held[i] for i in now]), bit)
            held.update({i | bit: (got, at) for at, i in enumerate(now)})
            bit //= 2
        rest = [i for i in held if i]
        got = swap_parts(joined([held[i] for i in rest]))
        others = {i: (got, at) for at, i in enumerate(rest)}
        return finish_gather(held, others, [rest], first)

    def chip_exchange(payloads):
        got = [payloads[0]] + [None] * (chips - 1)
        for kc in range(chips - 1, 0, -1):
            got[kc] = swap_inner(payloads[kc], 2 * kc)
        return got

    a_stacks, a_places = gather_by_piece(0, split)
    b_stacks, b_places = gather_joined(split, sections - split)

    picks = pl.pallas_call(
        functools.partial(pick_kernel, q),
        out_shape=shape(sections, k, k),
        in_specs=[smem, VMEM],
        out_specs=VMEM,
        scratch_shapes=[vmem((1, k), jnp.int32)],
        compiler_params=ROOM,
        cost_estimate=flat_cost(0, 2 * sections * k * k),
        name="picks",
    )(scalars, column_order.reshape(sections, k // LANES, LANES))

    from_sib = swap_inner(for_sib, 1)
    payloads = pl.pallas_call(
        pack_kernel,
        out_shape=[shape(2, 2, block, k)] * chips,
        in_specs=[smem, ANY, ANY],
        out_specs=[ANY] * chips,
        scratch_shapes=[vmem((2, 2, chips, block, k), BF16), pltpu.SemaphoreType.DMA((3,))],
        cost_estimate=flat_cost(0, 8 * rows * k),
        compiler_params=ROOM,
        name="pack",
    )(scalars, by_core, from_sib)
    pieces = chip_exchange(payloads)

    mm = 8 * m * k * k

    def mid(chunk):
        return pl.pallas_call(
            functools.partial(mid_kernel, n, q, rc, chunk, a_places, len(a_stacks)),
            out_shape=[shape(2, 2, rc, k)] * chips,
            in_specs=[smem] + [VMEM] * (1 + chips + len(a_stacks)),
            out_specs=[VMEM] * chips,
            scratch_shapes=[
                pltpu.VMEM((2, n, rc, k), BF16),
                pltpu.VMEM((2 * m, k), BF16),
                pltpu.VMEM((n, 2, rc, k), BF16),
            ],
            cost_estimate=flat_cost(3 * mm, 16 * k * k),
            compiler_params=ROOM,
        )(scalars, picks, *pieces, *a_stacks)

    branch = pl.pallas_call(
        functools.partial(turn_kernel, b_places, len(b_stacks)),
        out_shape=shape(2, k, k),
        in_specs=[smem] + [VMEM] * (1 + len(b_stacks)),
        out_specs=VMEM,
        cost_estimate=flat_cost(4 * k * k * k, 8 * k * k),
        compiler_params=ROOM,
        name="turn",
    )(scalars, picks, *b_stacks)

    def fin(chunk, arrived, prev):
        extra = [] if prev is None else [prev]
        n_in = 3 + chips
        return pl.pallas_call(
            functools.partial(fin_kernel, n, rc, chunk, bool(extra)),
            out_shape=shape(2, rows, k),
            in_specs=[smem] + [VMEM] * (n_in - 1) + [ANY] * len(extra),
            out_specs=ANY,
            scratch_shapes=[
                vmem((2, n, rc, k), BF16),
                vmem((2, n, rc, k), BF16),
                pltpu.SemaphoreType.DMA((3,)),
            ],
            input_output_aliases={n_in: 0} if extra else {},
            cost_estimate=flat_cost(mm, 8 * k * k),
            compiler_params=ROOM,
        )(scalars, branch, *arrived, *extra)

    result = None
    for chunk in range(CHUNKS):
        outs = mid(chunk)
        arrived = chip_exchange(outs)
        forwarded = pl.pallas_call(
            forward_kernel,
            out_shape=shape(chips, 2, rc, k),
            in_specs=[ANY] * chips,
            out_specs=ANY,
            scratch_shapes=[vmem((chips, 2, rc, k), BF16), pltpu.SemaphoreType.DMA((2,))],
            cost_estimate=flat_cost(0, 8 * m * k),
            compiler_params=ROOM,
        )(*arrived)
        arrived = arrived + [swap_inner(forwarded, 1)]
        result = fin(chunk, arrived, result)
    return result


def fits(n, n_parts, rows, k):
    power_of_two = n >= 8 and n & (n - 1) == 0
    return power_of_two and n_parts % 2 == 0 and k == n * LANES // 2 and rows % (n * CHUNKS * 16) == 0


def solution(mesh):
    n, n_parts = mesh.shape["inner"], mesh.shape["parts"]

    def body(stem_slab, branches, column_order):
        if not fits(n, n_parts, *stem_slab.shape[1:]):
            return plain(stem_slab, branches, column_order)
        return local(n, stem_slab, branches, column_order)

    in_specs = (P(None, ("parts", "inner"), None), P(None, None, "inner", None), P())
    out_specs = P(None, ("parts", "inner"), None)
    return jax.shard_map(body, mesh=mesh, in_specs=in_specs, out_specs=out_specs, check_vma=False)
```

time: 275 us -> 246 us (0.89)
  local copies, waits for them, and re-layouts: 74.9 us -> 1.94 us
  starting transfers between devices: 10.8 us -> 76.1 us
  Pallas kernels: 0 us -> 44.8 us
  matrix products: 20.8 us -> 0 us
  waiting for transfers between devices: 141 us -> 121 us
  other arithmetic: 13.7 us -> 0.07 us
  between operations: 13.4 us -> 0.53 us
    ppermute x0 -> x47, waiting for transfers between devices: none -> 121 us  [the longest x39 94.6 us: swap_inner(): return lax.ppermute(x, 'inner', [(i, i ^ mask) for i in range(n)])]
    all_to_all x2 -> x0, waiting for transfers between devices: 116 us -> none  [local(): lax.all_to_all(current, 'inner', split_axis=2, concat_axis=2, tiled=True)]
    ppermute x0 -> x47, starting transfers between devices: none -> 76.1 us  [the longest x39 68.6 us: swap_inner(): return lax.ppermute(x, 'inner', [(i, i ^ mask) for i in range(n)])]
    pallas_call x0 -> x15, Pallas kernels: none -> 44.8 us  [the longest x2 17.9 us: mid(): pl.pallas_call(functools.partial(mid_kernel, n, q, rc, chunk, a_places, l...]
    slice x11 -> x0, local copies, waits for them, and re-layouts: 40 us -> none  [the longest x6 25.1 us: add_block(): ordered[0]]
    all_gather x3 -> x0, waiting for transfers between devices: 23 us -> none  [folded(): lax.all_gather(branch_slice, 'inner', axis=1, tiled=True)]
    gather x3 -> x0, local copies, waits for them, and re-layouts: 22.4 us -> none  [folded(): ordered = jnp.take(slab, order_row, axis=2)]
    dot_general x12 -> x0, matrix products: 20.8 us -> none  [the longest x3 9.41 us: add_block(): jnp.dot(ordered[0], block_rows[0], preferred_element_type=jnp.float32)]
  transfers between devices with their start and end apart: 5 -> 47, of which waited for: 3 -> 25; matrix products, arithmetic and copies ran while one was open for 36% -> 0% of each run, Pallas kernels for 0% -> 16%
where the time goes in v1:
time: 246 us; the launch traced here: 245 us
  waiting for transfers between devices  121 us (49%)
  starting transfers between devices  76.1 us (31%)
  Pallas kernels  44.8 us (18%)
    ppermute x39, waiting for transfers between devices, swap_inner(): return lax.ppermute(x, 'inner', [(i, i ^ mask) for i in range(n)])  94.6 us
    ppermute x39, starting transfers between devices, swap_inner(): return lax.ppermute(x, 'inner', [(i, i ^ mask) for i in range(n)])  68.6 us
    ppermute x8, waiting for transfers between devices, swap_parts(): return lax.ppermute(x, 'parts', [(i, i ^ 1) for i in range(n_parts)])  26.6 us
    pallas_call x2, Pallas kernels, mid(): pl.pallas_call(functools.partial(mid_kernel, n, q, rc, chunk, a_places, l...  17.9 us
    pallas_call x2, Pallas kernels, fin(): pl.pallas_call(functools.partial(fin_kernel, n, rc, chunk, bool(extra)),...  7.73 us
    ppermute x8, starting transfers between devices, swap_parts(): return lax.ppermute(x, 'parts', [(i, i ^ 1) for i in range(n_parts)])  7.49 us
    pallas_call x5, Pallas kernels, joined(): pl.pallas_call(functools.partial(join_kernel, tuple(items)), out_shape=wh...  6.6 us
    pallas_call x1, Pallas kernels, local(): pl.pallas_call(functools.partial(turn_kernel, b_places, len(b_stacks)), o...  5.4 us
  transfers between devices with their start and end apart: 47, of which 25 were waited for; matrix products, arithmetic and copies ran while one was open for 0% of the time, Pallas kernels for 16%

profile of v1, /device:TPU:13, one launch (start us, length us, event | category | flops | bytes accessed | tf_op | source)
XLA Modules:
  0.0 244.6 jit_solution(18156922097862068538)
XLA Ops:
  0.0 1.0 dynamic-slice_bitcast_fusion
  1.0 1.4 collective-permute-start.16
  2.3 2.2 collective-permute-start.15
  4.8 9.3 %collective-permute-done.16.refs_1_.rest_10_ = bf16[2,64,1024]{2,1,0:T(8,128)(2,1)S(1)} collective-permute-done((bf16[2,64,1024]{2,1,0:T(8,128)(2,1)S(1)}, bf16[2,64,1024]{2,1,0:T(8,128)(2,1)S(1)}, u32[]{:S(2)}, u32[]{:S(2)}) %collective-permute-start.16) | collective-permute-done | bytes 262176 | tf_op jit(solution)/shard_map/ppermute | solution.py:237
  14.0 1.9 collective-permute-done.15.refs_0_.rest_8_
  16.2 1.2 collective-permute-start.20
  17.7 1.2 collective-permute-start.23
  18.9 2.3 collective-permute-done.17.refs_2_.rest_11_
  21.2 1.2 collective-permute-start.22
  22.4 0.9 collective-permute-start.24
  23.3 4.3 %collective-permute-done.21.refs_6_.rest_15_ = bf16[2,64,1024]{2,1,0:T(8,128)(2,1)S(1)} collective-permute-done((bf16[2,64,1024]{2,1,0:T(8,128)(2,1)S(1)}, bf16[2,64,1024]{2,1,0:T(8,128)(2,1)S(1)}, u32[]{:S(2)}, u32[]{:S(2)}) %collective-permute-start.21) | collective-permute-done | bytes 262176 | tf_op jit(solution)/shard_map/ppermute | solution.py:240
  27.6 5.6 %collective-permute-done.23.refs_8_.rest_17_ = bf16[2,64,1024]{2,1,0:T(8,128)(2,1)S(1)} collective-permute-done((bf16[2,64,1024]{2,1,0:T(8,128)(2,1)S(1)}, bf16[2,64,1024]{2,1,0:T(8,128)(2,1)S(1)}, u32[]{:S(2)}, u32[]{:S(2)}) %collective-permute-start.23) | collective-permute-done | bytes 262176 | tf_op jit(solution)/shard_map/ppermute | solution.py:240
  33.2 5.6 %collective-permute-done.22.refs_7_.rest_16_ = bf16[2,64,1024]{2,1,0:T(8,128)(2,1)S(1)} collective-permute-done((bf16[2,64,1024]{2,1,0:T(8,128)(2,1)S(1)}, bf16[2,64,1024]{2,1,0:T(8,128)(2,1)S(1)}, u32[]{:S(2)}, u32[]{:S(2)}) %collective-permute-start.22) | collective-permute-done | bytes 262176 | tf_op jit(solution)/shard_map/ppermute | solution.py:240
  38.8 5.6 %collective-permute-done.24.refs_9_.rest_18_ = bf16[2,64,1024]{2,1,0:T(8,128)(2,1)S(1)} collective-permute-done((bf16[2,64,1024]{2,1,0:T(8,128)(2,1)S(1)}, bf16[2,64,1024]{2,1,0:T(8,128)(2,1)S(1)}, u32[]{:S(2)}, u32[]{:S(2)}) %collective-permute-start.24) | collective-permute-done | bytes 262176 | tf_op jit(solution)/shard_map/ppermute | solution.py:240
  44.5 1.7 shard_map.40
  46.2 3.0 %collective-permute-start.25 = (bf16[10,2,64,1024]{3,2,1,0:T(8,128)(2,1)}, bf16[10,2,64,1024]{3,2,1,0:T(8,128)(2,1)}, u32[]{:S(2)}, u32[]{:S(2)}) collective-permute-start(bf16[10,2,64,1024]{3,2,1,0:T(8,128)(2,1)} %shard_map.40), channel_id=1, source_target_pairs={{0,1},{1,0},{2,3},{3,2},{4,5},{5,4},{6,7},{7,6},{8,9},{9,8},{10,11... | collective-permute-start | bytes 7864328 | tf_op jit(solution)/shard_map/ppermute | solution.py:237
  49.2 0.9 dynamic-slice_bitcast_fusion.1.refs_0_
  50.2 1.5 collective-permute-start
  51.8 6.3 %collective-permute-done.1.refs_2_.refs_1_.rest_2_ = bf16[1,64,1024]{2,1,0:T(8,128)(2,1)S(1)} collective-permute-done((bf16[1,64,1024]{2,1,0:T(8,128)(2,1)S(1)}, bf16[1,64,1024]{2,1,0:T(8,128)(2,1)S(1)}, u32[]{:S(2)}, u32[]{:S(2)}) %collective-permute-start.1) | collective-permute-done | bytes 131104 | tf_op jit(solution)/shard_map/ppermute | solution.py:237
  58.9 1.7 collective-permute-start.7
  60.6 1.6 collective-permute-done.2.refs_3_.refs_2_.rest_3_
  62.9 1.3 collective-permute-start.3
  64.5 2.3 collective-permute-start.6
  66.8 13.6 %collective-permute-done.26.refs_0_.rest_19_ = bf16[2,64,1024]{2,1,0:T(8,128)(2,1)S(1)} collective-permute-done((bf16[2,64,1024]{2,1,0:T(8,128)(2,1)S(1)}, bf16[2,64,1024]{2,1,0:T(8,128)(2,1)S(1)}, u32[]{:S(2)}, u32[]{:S(2)}) %collective-permute-start.26) | collective-permute-done | bytes 262176 | tf_op jit(solution)/shard_map/ppermute | solution.py:237
  80.4 1.2 collective-permute-start.27
  81.6 1.2 collective-permute-start.28
  82.8 2.8 %collective-permute-done.27.refs_1_.rest_21_ = bf16[2,64,1024]{2,1,0:T(8,128)(2,1)S(1)} collective-permute-done((bf16[2,64,1024]{2,1,0:T(8,128)(2,1)S(1)}, bf16[2,64,1024]{2,1,0:T(8,128)(2,1)S(1)}, u32[]{:S(2)}, u32[]{:S(2)}) %collective-permute-start.27) | collective-permute-done | bytes 262176 | tf_op jit(solution)/shard_map/ppermute | solution.py:237
  85.6 1.2 collective-permute-start.29
  86.8 1.4 shard_map.38
  88.5 5.4 %collective-permute-done.29.refs_3_.rest_23_ = bf16[2,64,1024]{2,1,0:T(8,128)(2,1)S(1)} collective-permute-done((bf16[2,64,1024]{2,1,0:T(8,128)(2,1)S(1)}, bf16[2,64,1024]{2,1,0:T(8,128)(2,1)S(1)}, u32[]{:S(2)}, u32[]{:S(2)}) %collective-permute-start.29) | collective-permute-done | bytes 262176 | tf_op jit(solution)/shard_map/ppermute | solution.py:240
  94.1 4.8 %collective-permute-start.30 = (bf16[4,2,64,1024]{3,2,1,0:T(8,128)(2,1)S(1)}, bf16[4,2,64,1024]{3,2,1,0:T(8,128)(2,1)S(1)}, u32[]{:S(2)}, u32[]{:S(2)}) collective-permute-start(bf16[4,2,64,1024]{3,2,1,0:T(8,128)(2,1)S(1)} %shard_map.41), channel_id=1, source_target_pairs={{0,1},{1,0},{2,3},{3,2},{4,5},{5,4},{6,7},{7,6},{8,9},{9,8},{10,11... | collective-permute-start | bytes 3145736 | tf_op jit(solution)/shard_map/ppermute | solution.py:237
  98.9 2.1 pack.1
  101.0 1.2 collective-permute-start.8
  102.2 6.7 %collective-permute-done.8.rest_1_ = bf16[2,2,32,1024]{3,2,1,0:T(8,128)(2,1)S(1)} collective-permute-done((bf16[2,2,32,1024]{3,2,1,0:T(8,128)(2,1)S(1)}, bf16[2,2,32,1024]{3,2,1,0:T(8,128)(2,1)S(1)}, u32[]{:S(2)}, u32[]{:S(2)}) %collective-permute-start.8) | collective-permute-done | bytes 262176 | tf_op jit(solution)/shard_map/ppermute | solution.py:237
  108.9 0.8 collective-permute-start.10
  109.7 1.8 collective-permute-start.11
  111.5 7.6 %collective-permute-done.10.rest_3_ = bf16[2,2,32,1024]{3,2,1,0:T(8,128)(2,1)S(1)} collective-permute-done((bf16[2,2,32,1024]{3,2,1,0:T(8,128)(2,1)S(1)}, bf16[2,2,32,1024]{3,2,1,0:T(8,128)(2,1)S(1)}, u32[]{:S(2)}, u32[]{:S(2)}) %collective-permute-start.10) | collective-permute-done | bytes 262176 | tf_op jit(solution)/shard_map/ppermute | solution.py:237
  119.1 3.7 %collective-permute-start.12 = (bf16[2,2,32,1024]{3,2,1,0:T(8,128)(2,1)S(1)}, bf16[2,2,32,1024]{3,2,1,0:T(8,128)(2,1)S(1)}, u32[]{:S(2)}, u32[]{:S(2)}) collective-permute-start(bf16[2,2,32,1024]{3,2,1,0:T(8,128)(2,1)S(1)} %get-tuple-element.34), channel_id=1, source_target_pairs={{0,10},{1,11},{2,8},{3,9},{4,14},{5,15},{6,12},{7,13},{8,2},{9,3},... | collective-permute-start | bytes 786440 | tf_op jit(solution)/shard_map/ppermute | solution.py:237
  123.6 1.2 collective-permute-start.14
  124.7 2.7 %shard_map.39 = bf16[14,1,64,1024]{3,2,1,0:T(8,128)(2,1)S(1)} custom-call(bf16[1,64,1024]{2,1,0:T(8,128)(2,1)S(1)} %collective-permute-done.refs_1_.refs_0_.rest_0_, bf16[1,64,1024]{2,1,0:T(8,128)(2,1)S(1)} %collective-permute-done.1.refs_2_.refs_1_.rest_2_, bf16[1,64,1024]{2,1,0:T(8,128)(2,1)S(1)} %collective-permute-done.2.refs_3_.refs_2_.rest_3_, ...), custom_call_target="tpu_custom_call" | custom-call | bytes 3670016 | tf_op jit(solution)/shard_map/pallas_call | solution.py:270
  127.4 12.2 %collective-permute-done.12.rest_5_ = bf16[2,2,32,1024]{3,2,1,0:T(8,128)(2,1)S(1)} collective-permute-done((bf16[2,2,32,1024]{3,2,1,0:T(8,128)(2,1)S(1)}, bf16[2,2,32,1024]{3,2,1,0:T(8,128)(2,1)S(1)}, u32[]{:S(2)}, u32[]{:S(2)}) %collective-permute-start.12) | collective-permute-done | bytes 262176 | tf_op jit(solution)/shard_map/ppermute | solution.py:237
  139.6 1.5 collective-permute-start.5
  141.1 3.0 %picks.1 = bf16[3,1024,1024]{2,1,0:T(8,128)(2,1)S(1)} custom-call(s32[2]{0:T(128)S(1)} %pad_add_fusion.scalars, s32[3,8,128]{2,1,0:T(8,128)S(1)} %bitcast.13), custom_call_target="tpu_custom_call" | custom-call | bytes 6291456 | tf_op jit(solution)/shard_map/picks/pallas_call | solution.py:345
  144.1 8.1 %collective-permute-done.13.rest_6_ = bf16[2,2,32,1024]{3,2,1,0:T(8,128)(2,1)S(1)} collective-permute-done((bf16[2,2,32,1024]{3,2,1,0:T(8,128)(2,1)S(1)}, bf16[2,2,32,1024]{3,2,1,0:T(8,128)(2,1)S(1)}, u32[]{:S(2)}, u32[]{:S(2)}) %collective-permute-start.13) | collective-permute-done | bytes 262176 | tf_op jit(solution)/shard_map/ppermute | solution.py:237
  152.2 5.6 %collective-permute-done.14.rest_7_ = bf16[2,2,32,1024]{3,2,1,0:T(8,128)(2,1)S(1)} collective-permute-done((bf16[2,2,32,1024]{3,2,1,0:T(8,128)(2,1)S(1)}, bf16[2,2,32,1024]{3,2,1,0:T(8,128)(2,1)S(1)}, u32[]{:S(2)}, u32[]{:S(2)}) %collective-permute-start.14) | collective-permute-done | bytes 262176 | tf_op jit(solution)/shard_map/ppermute | solution.py:237
  157.9 8.9 %shard_map.42 = (bf16[2,2,16,1024]{3,2,1,0:T(8,128)(2,1)S(1)}, bf16[2,2,16,1024]{3,2,1,0:T(8,128)(2,1)S(1)}, bf16[2,2,16,1024]{3,2,1,0:T(8,128)(2,1)S(1)}, bf16[...) custom-call(s32[2]{0:T(128)S(1)} %pad_add_fusion.scalars, ...), custom_call_target="tpu_custom_call" | custom-call | flops 6442450944 | bytes 16777216 | tf_op jit(solution)/shard_map/pallas_call | solution.py:372
  166.7 1.2 collective-permute-start.31
  168.0 1.5 collective-permute-start.33
  169.5 9.0 %shard_map.44 = (bf16[2,2,16,1024]{3,2,1,0:T(8,128)(2,1)S(1)}, bf16[2,2,16,1024]{3,2,1,0:T(8,128)(2,1)S(1)}, bf16[2,2,16,1024]{3,2,1,0:T(8,128)(2,1)S(1)}, bf16[...) custom-call(s32[2]{0:T(128)S(1)} %pad_add_fusion.scalars, ...), custom_call_target="tpu_custom_call" | custom-call | flops 6442450944 | bytes 16777216 | tf_op jit(solution)/shard_map/pallas_call | solution.py:372
  178.5 1.2 collective-permute-start.39
  179.7 1.5 collective-permute-start.41
  182.4 2.1 collective-permute-start.43
  184.5 0.9 collective-permute-start.44
  185.3 3.4 %collective-permute-start.45 = (bf16[2,2,16,1024]{3,2,1,0:T(8,128)(2,1)S(1)}, bf16[2,2,16,1024]{3,2,1,0:T(8,128)(2,1)S(1)}, u32[]{:S(2)}, u32[]{:S(2)}) collective-permute-start(bf16[2,2,16,1024]{3,2,1,0:T(8,128)(2,1)S(1)} %get-tuple-element.52), channel_id=1, source_target_pairs={{0,14},{1,15},{2,12},{3,13},{4,10},{5,11},{6,8},{7,9},{8,6},{9,7},... | collective-permute-start | bytes 393224 | tf_op jit(solution)/shard_map/ppermute | solution.py:237
  189.0 2.1 collective-permute-start.34
  191.8 14.7 %collective-permute-start.35 = (bf16[2,2,16,1024]{3,2,1,0:T(8,128)(2,1)S(1)}, bf16[2,2,16,1024]{3,2,1,0:T(8,128)(2,1)S(1)}, u32[]{:S(2)}, u32[]{:S(2)}) collective-permute-start(bf16[2,2,16,1024]{3,2,1,0:T(8,128)(2,1)S(1)} %get-tuple-element.42), channel_id=1, source_target_pairs={{0,10},{1,11},{2,8},{3,9},{4,14},{5,15},{6,12},{7,13},{8,2},{9,3},... | collective-permute-start | bytes 393224 | tf_op jit(solution)/shard_map/ppermute | solution.py:237
  207.5 9.1 %collective-permute-done.45.refs_7_.rest_7_ = bf16[2,2,16,1024]{3,2,1,0:T(8,128)(2,1)S(1)} collective-permute-done((bf16[2,2,16,1024]{3,2,1,0:T(8,128)(2,1)S(1)}, bf16[2,2,16,1024]{3,2,1,0:T(8,128)(2,1)S(1)}, u32[]{:S(2)}, u32[]{:S(2)}) %collective-permute-start.45) | collective-permute-done | bytes 131104 | tf_op jit(solution)/shard_map/ppermute | solution.py:237
  218.3 4.7 %collective-permute-start.46 = (bf16[8,2,16,1024]{3,2,1,0:T(8,128)(2,1)S(1)}, bf16[8,2,16,1024]{3,2,1,0:T(8,128)(2,1)S(1)}, u32[]{:S(2)}, u32[]{:S(2)}) collective-permute-start(bf16[8,2,16,1024]{3,2,1,0:T(8,128)(2,1)S(1)} %shard_map.45), channel_id=1, source_target_pairs={{0,1},{1,0},{2,3},{3,2},{4,5},{5,4},{6,7},{7,6},{8,9},{9,8},{10,11... | collective-permute-start | bytes 1572872 | tf_op jit(solution)/shard_map/ppermute | solution.py:237
  223.0 2.3 collective-permute-done.36.refs_6_.rest_6_
  225.3 2.5 %collective-permute-done.37.refs_7_.rest_7_ = bf16[2,2,16,1024]{3,2,1,0:T(8,128)(2,1)S(1)} collective-permute-done((bf16[2,2,16,1024]{3,2,1,0:T(8,128)(2,1)S(1)}, bf16[2,2,16,1024]{3,2,1,0:T(8,128)(2,1)S(1)}, u32[]{:S(2)}, u32[]{:S(2)}) %collective-permute-start.37) | collective-permute-done | bytes 131104 | tf_op jit(solution)/shard_map/ppermute | solution.py:237
  228.5 2.7 %collective-permute-start.38 = (bf16[8,2,16,1024]{3,2,1,0:T(8,128)(2,1)S(1)}, bf16[8,2,16,1024]{3,2,1,0:T(8,128)(2,1)S(1)}, u32[]{:S(2)}, u32[]{:S(2)}) collective-permute-start(bf16[8,2,16,1024]{3,2,1,0:T(8,128)(2,1)S(1)} %shard_map.43), channel_id=1, source_target_pairs={{0,1},{1,0},{2,3},{3,2},{4,5},{5,4},{6,7},{7,6},{8,9},{9,8},{10,11... | collective-permute-start | bytes 1572872 | tf_op jit(solution)/shard_map/ppermute | solution.py:237
  231.2 5.4 %turn.1.branch = bf16[2,1024,1024]{2,1,0:T(8,128)(2,1)S(1)} custom-call(s32[2]{0:T(128)S(1)} %pad_add_fusion.scalars, bf16[3,1024,1024]{2,1,0:T(8,128)(2,1)S(1)} %picks.1, bf16[1,64,1024]{2,1,0:T(8,128)(2,1)S(1)} %collective-permute-done.refs_1_.refs_0_.rest_0_, bf16[14,1,64,1024]{3,2,1,0:T(8,128)(2,1)S(1)} %collective-permute-done.5.rest_1_, ...), custom_call_target="tpu_custom_call" | custom-call | flops 4294967296 | bytes 8388608 | tf_op jit(solution)/shard_map/turn/pallas_call | solution.py:386
  236.6 3.9 %shard_map.46.rest_9_ = bf16[2,512,1024]{2,1,0:T(8,128)(2,1)} custom-call(s32[2]{0:T(128)S(1)} %pad_add_fusion.scalars, bf16[2,1024,1024]{2,1,0:T(8,128)(2,1)S(1)} %turn.1.branch, bf16[2,2,16,1024]{3,2,1,0:T(8,128)(2,1)S(1)} %get-tuple-element.45.refs_0_.rest_0_, bf16[2,2,16,1024]{3,2,1,0:T(8,128)(2,1)S(1)} %collective-permute-done.39.refs_1_.rest_1_, ...), custom_call_target="tpu_custom_call" | custom-call | flops 2147483648 | bytes 8388608 | tf_op jit(solution)/shard_map/pallas_call | solution.py:399
  240.5 3.9 %shard_map.47 = bf16[2,512,1024]{2,1,0:T(8,128)(2,1)} custom-call(s32[2]{0:T(128)S(1)} %pad_add_fusion.scalars, bf16[2,1024,1024]{2,1,0:T(8,128)(2,1)S(1)} %turn.1.branch, bf16[2,2,16,1024]{3,2,1,0:T(8,128)(2,1)S(1)} %get-tuple-element.37.refs_0_.rest_0_, ...), custom_call_target="tpu_custom_call", output_to_operand_aliasing={{}: (11, {})} | custom-call | flops 2147483648 | bytes 8388608 | tf_op jit(solution)/shard_map/pallas_call | solution.py:399
  (79 shorter events, 9.4 us)
Async XLA Ops:
  1.0 57.2 %copy-start = (bf16[2,512,1024]{2,1,0:T(8,128)(2,1)S(1)}, bf16[2,512,1024]{2,1,0:T(8,128)(2,1)}, u32[]{:S(2)}) copy-start(bf16[2,512,1024]{2,1,0:T(8,128)(2,1)} %param.3) | copy-start | bytes 6291460
  1.0 13.1 %collective-permute-start.16 = (bf16[2,64,1024]{2,1,0:T(8,128)(2,1)S(1)}, bf16[2,64,1024]{2,1,0:T(8,128)(2,1)S(1)}, u32[]{:S(2)}, u32[]{:S(2)}) collective-permute-start(bf16[2,64,1024]{2,1,0:T(8,128)(2,1)S(1)} %dynamic-slice_bitcast_fusion), channel_id=1, source_target_pairs={{0,12},{1,13},{2,14},{3,15},{4,8},{5,9},{6,10},{7,11},{8,4},{9,5},... | collective-permute-start | bytes 786440 | tf_op jit(solution)/shard_map/ppermute | solution.py:237
  2.3 13.6 %collective-permute-start.15 = (bf16[2,64,1024]{2,1,0:T(8,128)(2,1)S(1)}, bf16[2,64,1024]{2,1,0:T(8,128)(2,1)S(1)}, u32[]{:S(2)}, u32[]{:S(2)}) collective-permute-start(bf16[2,64,1024]{2,1,0:T(8,128)(2,1)S(1)} %dynamic-slice_bitcast_fusion), channel_id=1, source_target_pairs={{0,4},{1,5},{2,6},{3,7},{4,0},{5,1},{6,2},{7,3},{8,12},{9,13},{10,... | collective-permute-start | bytes 786440 | tf_op jit(solution)/shard_map/ppermute | solution.py:237
  4.5 13.1 %collective-permute-start.18 = (bf16[2,64,1024]{2,1,0:T(8,128)(2,1)S(1)}, bf16[2,64,1024]{2,1,0:T(8,128)(2,1)S(1)}, u32[]{:S(2)}, u32[]{:S(2)}) collective-permute-start(bf16[2,64,1024]{2,1,0:T(8,128)(2,1)S(1)} %dynamic-slice_bitcast_fusion), channel_id=1, source_target_pairs={{0,2},{1,3},{2,0},{3,1},{4,6},{5,7},{6,4},{7,5},{8,10},{9,11},{10,... | collective-permute-start | bytes 786440 | tf_op jit(solution)/shard_map/ppermute | solution.py:237
  14.0 7.1 %collective-permute-start.17 = (bf16[2,64,1024]{2,1,0:T(8,128)(2,1)S(1)}, bf16[2,64,1024]{2,1,0:T(8,128)(2,1)S(1)}, u32[]{:S(2)}, u32[]{:S(2)}) collective-permute-start(bf16[2,64,1024]{2,1,0:T(8,128)(2,1)S(1)} %collective-permute-done.16.refs_1_.rest_10_), channel_id=1, source_target_pairs={{0,4},{1,5},{2,6},{3,7},{4,0},{5,1},{6,2},{7,3},{8,12},{9,13},{10,... | collective-permute-start | bytes 786440 | tf_op jit(solution)/shard_map/ppermute | solution.py:237
  16.0 6.4 %collective-permute-start.19 = (bf16[2,64,1024]{2,1,0:T(8,128)(2,1)S(1)}, bf16[2,64,1024]{2,1,0:T(8,128)(2,1)S(1)}, u32[]{:S(2)}, u32[]{:S(2)}) collective-permute-start(bf16[2,64,1024]{2,1,0:T(8,128)(2,1)S(1)} %collective-permute-done.15.refs_0_.rest_8_), channel_id=1, source_target_pairs={{0,2},{1,3},{2,0},{3,1},{4,6},{5,7},{6,4},{7,5},{8,10},{9,11},{10,... | collective-permute-start | bytes 786440 | tf_op jit(solution)/shard_map/ppermute | solution.py:237
  16.2 7.1 %collective-permute-start.20 = (bf16[2,64,1024]{2,1,0:T(8,128)(2,1)S(1)}, bf16[2,64,1024]{2,1,0:T(8,128)(2,1)S(1)}, u32[]{:S(2)}, u32[]{:S(2)}) collective-permute-start(bf16[2,64,1024]{2,1,0:T(8,128)(2,1)S(1)} %collective-permute-done.15.refs_0_.rest_8_), channel_id=1, source_target_pairs={{0,16},{16,0},{1,17},{17,1},{2,18},{18,2},{3,19},{19,3},{4,20},{20... | collective-permute-start | bytes 786440 | tf_op jit(solution)/shard_map/ppermute | solution.py:240
  17.4 10.2 %collective-permute-start.21 = (bf16[2,64,1024]{2,1,0:T(8,128)(2,1)S(1)}, bf16[2,64,1024]{2,1,0:T(8,128)(2,1)S(1)}, u32[]{:S(2)}, u32[]{:S(2)}) collective-permute-start(bf16[2,64,1024]{2,1,0:T(8,128)(2,1)S(1)} %collective-permute-done.16.refs_1_.rest_10_), channel_id=1, source_target_pairs={{0,16},{16,0},{1,17},{17,1},{2,18},{18,2},{3,19},{19,3},{4,20},{20... | collective-permute-start | bytes 786440 | tf_op jit(solution)/shard_map/ppermute | solution.py:240
  17.7 15.6 %collective-permute-start.23 = (bf16[2,64,1024]{2,1,0:T(8,128)(2,1)S(1)}, bf16[2,64,1024]{2,1,0:T(8,128)(2,1)S(1)}, u32[]{:S(2)}, u32[]{:S(2)}) collective-permute-start(bf16[2,64,1024]{2,1,0:T(8,128)(2,1)S(1)} %collective-permute-done.18.refs_3_.rest_12_), channel_id=1, source_target_pairs={{0,16},{16,0},{1,17},{17,1},{2,18},{18,2},{3,19},{19,3},{4,20},{20... | collective-permute-start | bytes 786440 | tf_op jit(solution)/shard_map/ppermute | solution.py:240
  21.2 17.7 %collective-permute-start.22 = (bf16[2,64,1024]{2,1,0:T(8,128)(2,1)S(1)}, bf16[2,64,1024]{2,1,0:T(8,128)(2,1)S(1)}, u32[]{:S(2)}, u32[]{:S(2)}) collective-permute-start(bf16[2,64,1024]{2,1,0:T(8,128)(2,1)S(1)} %collective-permute-done.17.refs_2_.rest_11_), channel_id=1, source_target_pairs={{0,16},{16,0},{1,17},{17,1},{2,18},{18,2},{3,19},{19,3},{4,20},{20... | collective-permute-start | bytes 786440 | tf_op jit(solution)/shard_map/ppermute | solution.py:240
  22.4 23.8 %copy-start.1 = (bf16[2,64,1024]{2,1,0:T(8,128)(2,1)}, bf16[2,64,1024]{2,1,0:T(8,128)(2,1)S(1)}, u32[]{:S(2)}) copy-start(bf16[2,64,1024]{2,1,0:T(8,128)(2,1)S(1)} %collective-permute-done.19.refs_4_.rest_13_) | copy-start | bytes 786436
  22.4 22.1 %collective-permute-start.24 = (bf16[2,64,1024]{2,1,0:T(8,128)(2,1)S(1)}, bf16[2,64,1024]{2,1,0:T(8,128)(2,1)S(1)}, u32[]{:S(2)}, u32[]{:S(2)}) collective-permute-start(bf16[2,64,1024]{2,1,0:T(8,128)(2,1)S(1)} %collective-permute-done.19.refs_4_.rest_13_), channel_id=1, source_target_pairs={{0,16},{16,0},{1,17},{17,1},{2,18},{18,2},{3,19},{19,3},{4,20},{20... | collective-permute-start | bytes 786440 | tf_op jit(solution)/shard_map/ppermute | solution.py:240
  23.3 22.9 %copy-start.3 = (bf16[2,64,1024]{2,1,0:T(8,128)(2,1)}, bf16[2,64,1024]{2,1,0:T(8,128)(2,1)S(1)}, u32[]{:S(2)}) copy-start(bf16[2,64,1024]{2,1,0:T(8,128)(2,1)S(1)} %collective-permute-done.20.refs_5_.rest_14_) | copy-start | bytes 786436
  27.6 18.6 %copy-start.5 = (bf16[2,64,1024]{2,1,0:T(8,128)(2,1)}, bf16[2,64,1024]{2,1,0:T(8,128)(2,1)S(1)}, u32[]{:S(2)}) copy-start(bf16[2,64,1024]{2,1,0:T(8,128)(2,1)S(1)} %collective-permute-done.21.refs_6_.rest_15_) | copy-start | bytes 786436
  33.2 13.0 %copy-start.7 = (bf16[2,64,1024]{2,1,0:T(8,128)(2,1)}, bf16[2,64,1024]{2,1,0:T(8,128)(2,1)S(1)}, u32[]{:S(2)}) copy-start(bf16[2,64,1024]{2,1,0:T(8,128)(2,1)S(1)} %collective-permute-done.23.refs_8_.rest_17_) | copy-start | bytes 786436
  38.8 7.4 %copy-start.9 = (bf16[2,64,1024]{2,1,0:T(8,128)(2,1)}, bf16[2,64,1024]{2,1,0:T(8,128)(2,1)S(1)}, u32[]{:S(2)}) copy-start(bf16[2,64,1024]{2,1,0:T(8,128)(2,1)S(1)} %collective-permute-done.22.refs_7_.rest_16_) | copy-start | bytes 786436
  44.5 1.8 copy-start.11
  46.2 111.6 %collective-permute-start.25 = (bf16[10,2,64,1024]{3,2,1,0:T(8,128)(2,1)}, bf16[10,2,64,1024]{3,2,1,0:T(8,128)(2,1)}, u32[]{:S(2)}, u32[]{:S(2)}) collective-permute-start(bf16[10,2,64,1024]{3,2,1,0:T(8,128)(2,1)} %shard_map.40), channel_id=1, source_target_pairs={{0,1},{1,0},{2,3},{3,2},{4,5},{5,4},{6,7},{7,6},{8,9},{9,8},{10,11... | collective-permute-start | bytes 7864328 | tf_op jit(solution)/shard_map/ppermute | solution.py:237
  50.1 7.9 %collective-permute-start.1 = (bf16[1,64,1024]{2,1,0:T(8,128)(2,1)S(1)}, bf16[1,64,1024]{2,1,0:T(8,128)(2,1)S(1)}, u32[]{:S(2)}, u32[]{:S(2)}) collective-permute-start(bf16[1,64,1024]{2,1,0:T(8,128)(2,1)S(1)} %dynamic-slice_bitcast_fusion.1.refs_0_), channel_id=1, source_target_pairs={{0,12},{1,13},{2,14},{3,15},{4,8},{5,9},{6,10},{7,11},{8,4},{9,5},... | collective-permute-start | bytes 393224 | tf_op jit(solution)/shard_map/ppermute | solution.py:237
  50.2 10.4 %collective-permute-start = (bf16[1,64,1024]{2,1,0:T(8,128)(2,1)S(1)}, bf16[1,64,1024]{2,1,0:T(8,128)(2,1)S(1)}, u32[]{:S(2)}, u32[]{:S(2)}) collective-permute-start(bf16[1,64,1024]{2,1,0:T(8,128)(2,1)S(1)} %dynamic-slice_bitcast_fusion.1.refs_0_), channel_id=1, source_target_pairs={{0,4},{1,5},{2,6},{3,7},{4,0},{5,1},{6,2},{7,3},{8,12},{9,13},{10,... | collective-permute-start | bytes 393224 | tf_op jit(solution)/shard_map/ppermute | solution.py:237
  58.0 4.2 %collective-permute-start.2 = (bf16[1,64,1024]{2,1,0:T(8,128)(2,1)S(1)}, bf16[1,64,1024]{2,1,0:T(8,128)(2,1)S(1)}, u32[]{:S(2)}, u32[]{:S(2)}) collective-permute-start(bf16[1,64,1024]{2,1,0:T(8,128)(2,1)S(1)} %collective-permute-done.1.refs_2_.refs_1_.rest_2_), channel_id=1, source_target_pairs={{0,4},{1,5},{2,6},{3,7},{4,0},{5,1},{6,2},{7,3},{8,12},{9,13},{10,... | collective-permute-start | bytes 393224 | tf_op jit(solution)/shard_map/ppermute | solution.py:237
  58.2 6.3 %copy-start.13 = (bf16[3,2,64,1024]{3,2,1,0:T(8,128)(2,1)S(1)}, bf16[3,2,64,1024]{3,2,1,0:T(8,128)(2,1)}, u32[]{:S(2)}) copy-start(bf16[3,2,64,1024]{3,2,1,0:T(8,128)(2,1)} %rest_24_.3) | copy-start | bytes 2359300
  58.9 39.9 %collective-permute-start.7 = (bf16[2,8,32,1024]{3,2,1,0:T(8,128)(2,1)S(1)}, bf16[2,8,32,1024]{3,2,1,0:T(8,128)(2,1)S(1)}, u32[]{:S(2)}, u32[]{:S(2)}) collective-permute-start(bf16[2,8,32,1024]{3,2,1,0:T(8,128)(2,1)S(1)} %prep.1), channel_id=1, source_target_pairs={{0,1},{1,0},{2,3},{3,2},{4,5},{5,4},{6,7},{7,6},{8,9},{9,8},{10,11... | collective-permute-start | bytes 3145736 | tf_op jit(solution)/shard_map/ppermute | solution.py:237
  62.9 18.7 %collective-permute-start.3 = (bf16[4,1,64,1024]{3,2,1,0:T(8,128)(2,1)S(1)}, bf16[4,1,64,1024]{3,2,1,0:T(8,128)(2,1)S(1)}, u32[]{:S(2)}, u32[]{:S(2)}) collective-permute-start(bf16[4,1,64,1024]{3,2,1,0:T(8,128)(2,1)S(1)} %shard_map.37), channel_id=1, source_target_pairs={{0,2},{1,3},{2,0},{3,1},{4,6},{5,7},{6,4},{7,5},{8,10},{9,11},{10,... | collective-permute-start | bytes 1572872 | tf_op jit(solution)/shard_map/ppermute | solution.py:237
  64.2 16.1 %collective-permute-start.26 = (bf16[2,64,1024]{2,1,0:T(8,128)(2,1)S(1)}, bf16[2,64,1024]{2,1,0:T(8,128)(2,1)S(1)}, u32[]{:S(2)}, u32[]{:S(2)}) collective-permute-start(bf16[2,64,1024]{2,1,0:T(8,128)(2,1)S(1)} %collective-permute-done.16.refs_1_.rest_10_), channel_id=1, source_target_pairs={{0,2},{1,3},{2,0},{3,1},{4,6},{5,7},{6,4},{7,5},{8,10},{9,11},{10,... | collective-permute-start | bytes 786440 | tf_op jit(solution)/shard_map/ppermute | solution.py:237
  64.5 37.7 %collective-permute-start.6 = (bf16[3,2,64,1024]{3,2,1,0:T(8,128)(2,1)S(1)}, bf16[3,2,64,1024]{3,2,1,0:T(8,128)(2,1)S(1)}, u32[]{:S(2)}, u32[]{:S(2)}) collective-permute-start(bf16[3,2,64,1024]{3,2,1,0:T(8,128)(2,1)S(1)} %copy-done.13), channel_id=1, source_target_pairs={{0,1},{1,0},{2,3},{3,2},{4,5},{5,4},{6,7},{7,6},{8,9},{9,8},{10,11... | collective-permute-start | bytes 2359304 | tf_op jit(solution)/shard_map/ppermute | solution.py:237
  80.4 5.2 %collective-permute-start.27 = (bf16[2,64,1024]{2,1,0:T(8,128)(2,1)S(1)}, bf16[2,64,1024]{2,1,0:T(8,128)(2,1)S(1)}, u32[]{:S(2)}, u32[]{:S(2)}) collective-permute-start(bf16[2,64,1024]{2,1,0:T(8,128)(2,1)S(1)} %collective-permute-done.17.refs_2_.rest_11_), channel_id=1, source_target_pairs={{0,2},{1,3},{2,0},{3,1},{4,6},{5,7},{6,4},{7,5},{8,10},{9,11},{10,... | collective-permute-start | bytes 786440 | tf_op jit(solution)/shard_map/ppermute | solution.py:237
  81.6 6.6 %collective-permute-start.28 = (bf16[2,64,1024]{2,1,0:T(8,128)(2,1)S(1)}, bf16[2,64,1024]{2,1,0:T(8,128)(2,1)S(1)}, u32[]{:S(2)}, u32[]{:S(2)}) collective-permute-start(bf16[2,64,1024]{2,1,0:T(8,128)(2,1)S(1)} %collective-permute-done.26.refs_0_.rest_19_), channel_id=1, source_target_pairs={{0,16},{16,0},{1,17},{17,1},{2,18},{18,2},{3,19},{19,3},{4,20},{20... | collective-permute-start | bytes 786440 | tf_op jit(solution)/shard_map/ppermute | solution.py:240
  85.6 8.3 %collective-permute-start.29 = (bf16[2,64,1024]{2,1,0:T(8,128)(2,1)S(1)}, bf16[2,64,1024]{2,1,0:T(8,128)(2,1)S(1)}, u32[]{:S(2)}, u32[]{:S(2)}) collective-permute-start(bf16[2,64,1024]{2,1,0:T(8,128)(2,1)S(1)} %collective-permute-done.27.refs_1_.rest_21_), channel_id=1, source_target_pairs={{0,16},{16,0},{1,17},{17,1},{2,18},{18,2},{3,19},{19,3},{4,20},{20... | collective-permute-start | bytes 786440 | tf_op jit(solution)/shard_map/ppermute | solution.py:240
  88.2 35.4 %collective-permute-start.4 = (bf16[7,1,64,1024]{3,2,1,0:T(8,128)(2,1)S(1)}, bf16[7,1,64,1024]{3,2,1,0:T(8,128)(2,1)S(1)}, u32[]{:S(2)}, u32[]{:S(2)}) collective-permute-start(bf16[7,1,64,1024]{3,2,1,0:T(8,128)(2,1)S(1)} %shard_map.38), channel_id=1, source_target_pairs={{0,16},{16,0},{1,17},{17,1},{2,18},{18,2},{3,19},{19,3},{4,20},{20... | collective-permute-start | bytes 2752520 | tf_op jit(solution)/shard_map/ppermute | solution.py:240
  94.1 63.7 %collective-permute-start.30 = (bf16[4,2,64,1024]{3,2,1,0:T(8,128)(2,1)S(1)}, bf16[4,2,64,1024]{3,2,1,0:T(8,128)(2,1)S(1)}, u32[]{:S(2)}, u32[]{:S(2)}) collective-permute-start(bf16[4,2,64,1024]{3,2,1,0:T(8,128)(2,1)S(1)} %shard_map.41), channel_id=1, source_target_pairs={{0,1},{1,0},{2,3},{3,2},{4,5},{5,4},{6,7},{7,6},{8,9},{9,8},{10,11... | collective-permute-start | bytes 3145736 | tf_op jit(solution)/shard_map/ppermute | solution.py:237
  100.9 40.1 %copy-start.14 = (s32[3,1024]{1,0:T(4,128)S(1)}, s32[3,1024]{1,0:T(4,128)}, u32[]{:S(2)}) copy-start(s32[3,1024]{1,0:T(4,128)} %param.5) | copy-start | bytes 36868
  101.0 7.9 %collective-permute-start.8 = (bf16[2,2,32,1024]{3,2,1,0:T(8,128)(2,1)S(1)}, bf16[2,2,32,1024]{3,2,1,0:T(8,128)(2,1)S(1)}, u32[]{:S(2)}, u32[]{:S(2)}) collective-permute-start(bf16[2,2,32,1024]{3,2,1,0:T(8,128)(2,1)S(1)} %get-tuple-element.30), channel_id=1, source_target_pairs={{0,2},{1,3},{2,0},{3,1},{4,6},{5,7},{6,4},{7,5},{8,10},{9,11},{10,... | collective-permute-start | bytes 786440 | tf_op jit(solution)/shard_map/ppermute | solution.py:237
  102.2 7.6 %collective-permute-start.9 = (bf16[2,2,32,1024]{3,2,1,0:T(8,128)(2,1)S(1)}, bf16[2,2,32,1024]{3,2,1,0:T(8,128)(2,1)S(1)}, u32[]{:S(2)}, u32[]{:S(2)}) collective-permute-start(bf16[2,2,32,1024]{3,2,1,0:T(8,128)(2,1)S(1)} %get-tuple-element.31), channel_id=1, source_target_pairs={{0,4},{1,5},{2,6},{3,7},{4,0},{5,1},{6,2},{7,3},{8,12},{9,13},{10,... | collective-permute-start | bytes 786440 | tf_op jit(solution)/shard_map/ppermute | solution.py:237
  108.9 10.3 %collective-permute-start.10 = (bf16[2,2,32,1024]{3,2,1,0:T(8,128)(2,1)S(1)}, bf16[2,2,32,1024]{3,2,1,0:T(8,128)(2,1)S(1)}, u32[]{:S(2)}, u32[]{:S(2)}) collective-permute-start(bf16[2,2,32,1024]{3,2,1,0:T(8,128)(2,1)S(1)} %get-tuple-element.32), channel_id=1, source_target_pairs={{0,6},{1,7},{2,4},{3,5},{4,2},{5,3},{6,0},{7,1},{8,14},{9,15},{10,... | collective-permute-start | bytes 786440 | tf_op jit(solution)/shard_map/ppermute | solution.py:237
  109.7 13.1 %collective-permute-start.11 = (bf16[2,2,32,1024]{3,2,1,0:T(8,128)(2,1)S(1)}, bf16[2,2,32,1024]{3,2,1,0:T(8,128)(2,1)S(1)}, u32[]{:S(2)}, u32[]{:S(2)}) collective-permute-start(bf16[2,2,32,1024]{3,2,1,0:T(8,128)(2,1)S(1)} %get-tuple-element.33), channel_id=1, source_target_pairs={{0,8},{1,9},{2,10},{3,11},{4,12},{5,13},{6,14},{7,15},{8,0},{9,1},... | collective-permute-start | bytes 786440 | tf_op jit(solution)/shard_map/ppermute | solution.py:237
  119.1 20.4 %collective-permute-start.12 = (bf16[2,2,32,1024]{3,2,1,0:T(8,128)(2,1)S(1)}, bf16[2,2,32,1024]{3,2,1,0:T(8,128)(2,1)S(1)}, u32[]{:S(2)}, u32[]{:S(2)}) collective-permute-start(bf16[2,2,32,1024]{3,2,1,0:T(8,128)(2,1)S(1)} %get-tuple-element.34), channel_id=1, source_target_pairs={{0,10},{1,11},{2,8},{3,9},{4,14},{5,15},{6,12},{7,13},{8,2},{9,3},... | collective-permute-start | bytes 786440 | tf_op jit(solution)/shard_map/ppermute | solution.py:237
  122.8 29.3 %collective-permute-start.13 = (bf16[2,2,32,1024]{3,2,1,0:T(8,128)(2,1)S(1)}, bf16[2,2,32,1024]{3,2,1,0:T(8,128)(2,1)S(1)}, u32[]{:S(2)}, u32[]{:S(2)}) collective-permute-start(bf16[2,2,32,1024]{3,2,1,0:T(8,128)(2,1)S(1)} %get-tuple-element.35), channel_id=1, source_target_pairs={{0,12},{1,13},{2,14},{3,15},{4,8},{5,9},{6,10},{7,11},{8,4},{9,5},... | collective-permute-start | bytes 786440 | tf_op jit(solution)/shard_map/ppermute | solution.py:237
  123.6 34.2 %collective-permute-start.14 = (bf16[2,2,32,1024]{3,2,1,0:T(8,128)(2,1)S(1)}, bf16[2,2,32,1024]{3,2,1,0:T(8,128)(2,1)S(1)}, u32[]{:S(2)}, u32[]{:S(2)}) collective-permute-start(bf16[2,2,32,1024]{3,2,1,0:T(8,128)(2,1)S(1)} %get-tuple-element.36), channel_id=1, source_target_pairs={{0,14},{1,15},{2,12},{3,13},{4,10},{5,11},{6,8},{7,9},{8,6},{9,7},... | collective-permute-start | bytes 786440 | tf_op jit(solution)/shard_map/ppermute | solution.py:237
  139.6 91.6 %collective-permute-start.5 = (bf16[14,1,64,1024]{3,2,1,0:T(8,128)(2,1)S(1)}, bf16[14,1,64,1024]{3,2,1,0:T(8,128)(2,1)S(1)}, u32[]{:S(2)}, u32[]{:S(2)}) collective-permute-start(bf16[14,1,64,1024]{3,2,1,0:T(8,128)(2,1)S(1)} %shard_map.39), channel_id=1, source_target_pairs={{0,1},{1,0},{2,3},{3,2},{4,5},{5,4},{6,7},{7,6},{8,9},{9,8},{10,11... | collective-permute-start | bytes 5505032 | tf_op jit(solution)/shard_map/ppermute | solution.py:237
  141.0 16.8 %copy-start.2 = (bf16[2,64,1024]{2,1,0:T(8,128)(2,1)S(1)}, bf16[2,64,1024]{2,1,0:T(8,128)(2,1)}, u32[]{:S(2)}) copy-start(bf16[2,64,1024]{2,1,0:T(8,128)(2,1)} %copy-done.1) | copy-start | bytes 786436
  141.1 16.8 %copy-start.4 = (bf16[2,64,1024]{2,1,0:T(8,128)(2,1)S(1)}, bf16[2,64,1024]{2,1,0:T(8,128)(2,1)}, u32[]{:S(2)}) copy-start(bf16[2,64,1024]{2,1,0:T(8,128)(2,1)} %copy-done.3) | copy-start | bytes 786436
  141.1 16.8 %copy-start.6 = (bf16[2,64,1024]{2,1,0:T(8,128)(2,1)S(1)}, bf16[2,64,1024]{2,1,0:T(8,128)(2,1)}, u32[]{:S(2)}) copy-start(bf16[2,64,1024]{2,1,0:T(8,128)(2,1)} %copy-done.5) | copy-start | bytes 786436
  141.1 16.8 %copy-start.8 = (bf16[2,64,1024]{2,1,0:T(8,128)(2,1)S(1)}, bf16[2,64,1024]{2,1,0:T(8,128)(2,1)}, u32[]{:S(2)}) copy-start(bf16[2,64,1024]{2,1,0:T(8,128)(2,1)} %copy-done.7) | copy-start | bytes 786436
  141.1 16.8 %copy-start.10 = (bf16[2,64,1024]{2,1,0:T(8,128)(2,1)S(1)}, bf16[2,64,1024]{2,1,0:T(8,128)(2,1)}, u32[]{:S(2)}) copy-start(bf16[2,64,1024]{2,1,0:T(8,128)(2,1)} %copy-done.9) | copy-start | bytes 786436
  141.1 16.8 %copy-start.12 = (bf16[2,64,1024]{2,1,0:T(8,128)(2,1)S(1)}, bf16[2,64,1024]{2,1,0:T(8,128)(2,1)}, u32[]{:S(2)}) copy-start(bf16[2,64,1024]{2,1,0:T(8,128)(2,1)} %copy-done.11) | copy-start | bytes 786436
  166.7 13.0 %collective-permute-start.31 = (bf16[2,2,16,1024]{3,2,1,0:T(8,128)(2,1)S(1)}, bf16[2,2,16,1024]{3,2,1,0:T(8,128)(2,1)S(1)}, u32[]{:S(2)}, u32[]{:S(2)}) collective-permute-start(bf16[2,2,16,1024]{3,2,1,0:T(8,128)(2,1)S(1)} %get-tuple-element.38), channel_id=1, source_target_pairs={{0,2},{1,3},{2,0},{3,1},{4,6},{5,7},{6,4},{7,5},{8,10},{9,11},{10,... | collective-permute-start | bytes 393224 | tf_op jit(solution)/shard_map/ppermute | solution.py:237
  168.0 11.8 %collective-permute-start.32 = (bf16[2,2,16,1024]{3,2,1,0:T(8,128)(2,1)S(1)}, bf16[2,2,16,1024]{3,2,1,0:T(8,128)(2,1)S(1)}, u32[]{:S(2)}, u32[]{:S(2)}) collective-permute-start(bf16[2,2,16,1024]{3,2,1,0:T(8,128)(2,1)S(1)} %get-tuple-element.39), channel_id=1, source_target_pairs={{0,4},{1,5},{2,6},{3,7},{4,0},{5,1},{6,2},{7,3},{8,12},{9,13},{10,... | collective-permute-start | bytes 393224 | tf_op jit(solution)/shard_map/ppermute | solution.py:237
  168.0 13.3 %collective-permute-start.33 = (bf16[2,2,16,1024]{3,2,1,0:T(8,128)(2,1)S(1)}, bf16[2,2,16,1024]{3,2,1,0:T(8,128)(2,1)S(1)}, u32[]{:S(2)}, u32[]{:S(2)}) collective-permute-start(bf16[2,2,16,1024]{3,2,1,0:T(8,128)(2,1)S(1)} %get-tuple-element.40), channel_id=1, source_target_pairs={{0,6},{1,7},{2,4},{3,5},{4,2},{5,3},{6,0},{7,1},{8,14},{9,15},{10,... | collective-permute-start | bytes 393224 | tf_op jit(solution)/shard_map/ppermute | solution.py:237
  178.5 3.9 %collective-permute-start.39 = (bf16[2,2,16,1024]{3,2,1,0:T(8,128)(2,1)S(1)}, bf16[2,2,16,1024]{3,2,1,0:T(8,128)(2,1)S(1)}, u32[]{:S(2)}, u32[]{:S(2)}) collective-permute-start(bf16[2,2,16,1024]{3,2,1,0:T(8,128)(2,1)S(1)} %get-tuple-element.46), channel_id=1, source_target_pairs={{0,2},{1,3},{2,0},{3,1},{4,6},{5,7},{6,4},{7,5},{8,10},{9,11},{10,... | collective-permute-start | bytes 393224 | tf_op jit(solution)/shard_map/ppermute | solution.py:237
  179.7 4.7 %collective-permute-start.40 = (bf16[2,2,16,1024]{3,2,1,0:T(8,128)(2,1)S(1)}, bf16[2,2,16,1024]{3,2,1,0:T(8,128)(2,1)S(1)}, u32[]{:S(2)}, u32[]{:S(2)}) collective-permute-start(bf16[2,2,16,1024]{3,2,1,0:T(8,128)(2,1)S(1)} %get-tuple-element.47), channel_id=1, source_target_pairs={{0,4},{1,5},{2,6},{3,7},{4,0},{5,1},{6,2},{7,3},{8,12},{9,13},{10,... | collective-permute-start | bytes 393224 | tf_op jit(solution)/shard_map/ppermute | solution.py:237
  179.7 5.6 %collective-permute-start.41 = (bf16[2,2,16,1024]{3,2,1,0:T(8,128)(2,1)S(1)}, bf16[2,2,16,1024]{3,2,1,0:T(8,128)(2,1)S(1)}, u32[]{:S(2)}, u32[]{:S(2)}) collective-permute-start(bf16[2,2,16,1024]{3,2,1,0:T(8,128)(2,1)S(1)} %get-tuple-element.48), channel_id=1, source_target_pairs={{0,6},{1,7},{2,4},{3,5},{4,2},{5,3},{6,0},{7,1},{8,14},{9,15},{10,... | collective-permute-start | bytes 393224 | tf_op jit(solution)/shard_map/ppermute | solution.py:237
  181.2 7.8 %collective-permute-start.42 = (bf16[2,2,16,1024]{3,2,1,0:T(8,128)(2,1)S(1)}, bf16[2,2,16,1024]{3,2,1,0:T(8,128)(2,1)S(1)}, u32[]{:S(2)}, u32[]{:S(2)}) collective-permute-start(bf16[2,2,16,1024]{3,2,1,0:T(8,128)(2,1)S(1)} %get-tuple-element.49), channel_id=1, source_target_pairs={{0,8},{1,9},{2,10},{3,11},{4,12},{5,13},{6,14},{7,15},{8,0},{9,1},... | collective-permute-start | bytes 393224 | tf_op jit(solution)/shard_map/ppermute | solution.py:237
  182.4 9.4 %collective-permute-start.43 = (bf16[2,2,16,1024]{3,2,1,0:T(8,128)(2,1)S(1)}, bf16[2,2,16,1024]{3,2,1,0:T(8,128)(2,1)S(1)}, u32[]{:S(2)}, u32[]{:S(2)}) collective-permute-start(bf16[2,2,16,1024]{3,2,1,0:T(8,128)(2,1)S(1)} %get-tuple-element.50), channel_id=1, source_target_pairs={{0,10},{1,11},{2,8},{3,9},{4,14},{5,15},{6,12},{7,13},{8,2},{9,3},... | collective-permute-start | bytes 393224 | tf_op jit(solution)/shard_map/ppermute | solution.py:237
  184.5 22.5 %collective-permute-start.44 = (bf16[2,2,16,1024]{3,2,1,0:T(8,128)(2,1)S(1)}, bf16[2,2,16,1024]{3,2,1,0:T(8,128)(2,1)S(1)}, u32[]{:S(2)}, u32[]{:S(2)}) collective-permute-start(bf16[2,2,16,1024]{3,2,1,0:T(8,128)(2,1)S(1)} %get-tuple-element.51), channel_id=1, source_target_pairs={{0,12},{1,13},{2,14},{3,15},{4,8},{5,9},{6,10},{7,11},{8,4},{9,5},... | collective-permute-start | bytes 393224 | tf_op jit(solution)/shard_map/ppermute | solution.py:237
  185.3 31.2 %collective-permute-start.45 = (bf16[2,2,16,1024]{3,2,1,0:T(8,128)(2,1)S(1)}, bf16[2,2,16,1024]{3,2,1,0:T(8,128)(2,1)S(1)}, u32[]{:S(2)}, u32[]{:S(2)}) collective-permute-start(bf16[2,2,16,1024]{3,2,1,0:T(8,128)(2,1)S(1)} %get-tuple-element.52), channel_id=1, source_target_pairs={{0,14},{1,15},{2,12},{3,13},{4,10},{5,11},{6,8},{7,9},{8,6},{9,7},... | collective-permute-start | bytes 393224 | tf_op jit(solution)/shard_map/ppermute | solution.py:237
  189.0 29.3 %collective-permute-start.34 = (bf16[2,2,16,1024]{3,2,1,0:T(8,128)(2,1)S(1)}, bf16[2,2,16,1024]{3,2,1,0:T(8,128)(2,1)S(1)}, u32[]{:S(2)}, u32[]{:S(2)}) collective-permute-start(bf16[2,2,16,1024]{3,2,1,0:T(8,128)(2,1)S(1)} %get-tuple-element.41), channel_id=1, source_target_pairs={{0,8},{1,9},{2,10},{3,11},{4,12},{5,13},{6,14},{7,15},{8,0},{9,1},... | collective-permute-start | bytes 393224 | tf_op jit(solution)/shard_map/ppermute | solution.py:237
  191.8 31.2 %collective-permute-start.35 = (bf16[2,2,16,1024]{3,2,1,0:T(8,128)(2,1)S(1)}, bf16[2,2,16,1024]{3,2,1,0:T(8,128)(2,1)S(1)}, u32[]{:S(2)}, u32[]{:S(2)}) collective-permute-start(bf16[2,2,16,1024]{3,2,1,0:T(8,128)(2,1)S(1)} %get-tuple-element.42), channel_id=1, source_target_pairs={{0,10},{1,11},{2,8},{3,9},{4,14},{5,15},{6,12},{7,13},{8,2},{9,3},... | collective-permute-start | bytes 393224 | tf_op jit(solution)/shard_map/ppermute | solution.py:237
  207.0 18.3 %collective-permute-start.36 = (bf16[2,2,16,1024]{3,2,1,0:T(8,128)(2,1)S(1)}, bf16[2,2,16,1024]{3,2,1,0:T(8,128)(2,1)S(1)}, u32[]{:S(2)}, u32[]{:S(2)}) collective-permute-start(bf16[2,2,16,1024]{3,2,1,0:T(8,128)(2,1)S(1)} %get-tuple-element.43), channel_id=1, source_target_pairs={{0,12},{1,13},{2,14},{3,15},{4,8},{5,9},{6,10},{7,11},{8,4},{9,5},... | collective-permute-start | bytes 393224 | tf_op jit(solution)/shard_map/ppermute | solution.py:237
  216.6 11.2 %collective-permute-start.37 = (bf16[2,2,16,1024]{3,2,1,0:T(8,128)(2,1)S(1)}, bf16[2,2,16,1024]{3,2,1,0:T(8,128)(2,1)S(1)}, u32[]{:S(2)}, u32[]{:S(2)}) collective-permute-start(bf16[2,2,16,1024]{3,2,1,0:T(8,128)(2,1)S(1)} %get-tuple-element.44), channel_id=1, source_target_pairs={{0,14},{1,15},{2,12},{3,13},{4,10},{5,11},{6,8},{7,9},{8,6},{9,7},... | collective-permute-start | bytes 393224 | tf_op jit(solution)/shard_map/ppermute | solution.py:237
  218.3 18.4 %collective-permute-start.46 = (bf16[8,2,16,1024]{3,2,1,0:T(8,128)(2,1)S(1)}, bf16[8,2,16,1024]{3,2,1,0:T(8,128)(2,1)S(1)}, u32[]{:S(2)}, u32[]{:S(2)}) collective-permute-start(bf16[8,2,16,1024]{3,2,1,0:T(8,128)(2,1)S(1)} %shard_map.45), channel_id=1, source_target_pairs={{0,1},{1,0},{2,3},{3,2},{4,5},{5,4},{6,7},{7,6},{8,9},{9,8},{10,11... | collective-permute-start | bytes 1572872 | tf_op jit(solution)/shard_map/ppermute | solution.py:237
  228.5 12.0 %collective-permute-start.38 = (bf16[8,2,16,1024]{3,2,1,0:T(8,128)(2,1)S(1)}, bf16[8,2,16,1024]{3,2,1,0:T(8,128)(2,1)S(1)}, u32[]{:S(2)}, u32[]{:S(2)}) collective-permute-start(bf16[8,2,16,1024]{3,2,1,0:T(8,128)(2,1)S(1)} %shard_map.43), channel_id=1, source_target_pairs={{0,1},{1,0},{2,3},{3,2},{4,5},{5,4},{6,7},{7,6},{8,9},{9,8},{10,11... | collective-permute-start | bytes 1572872 | tf_op jit(solution)/shard_map/ppermute | solution.py:237

commit v2 on v1

--- a/solution.py
+++ b/solution.py
@@ -45,26 +45,18 @@
     pltpu.make_async_copy(ref, ref, sem).wait()
 
 
-def branch_tile(places, refs, section, mine, columns):
+def branch_rows(places, refs, section, mine, columns, half):
     rows = {}
-    for at, item, half, j, first in places:
+    for at, item, own_half, j, first in places:
         ref = refs[at] if item is None else refs[at].at[item]
-        if half is None:
-            rows[0, j] = ref[first + section, mine, :, columns]
-            rows[1, j] = ref[first + section, 1 - mine, :, columns]
-        else:
-            rows[half, j] = ref[section, :, columns]
-    return [jnp.concatenate([rows[half, j] for j in range(len(rows) // 2)], axis=0) for half in (0, 1)]
-
-
-def product_tile(x_ref, w_real, w_imag):
-    m = x_ref.shape[0] // 2
-    by_real = jnp.dot(x_ref[...], w_real, preferred_element_type=F32)
-    by_imag = jnp.dot(x_ref[...], w_imag, preferred_element_type=F32)
-    return by_real[:m] - by_imag[m:], by_imag[:m] + by_real[m:]
-
-
-def product_tile_halves(x_ref, w_mine, w_other, mine):
+        if own_half is None:
+            rows[j] = ref[first + section, 1 - mine if half else mine, :, columns]
+        elif own_half == half:
+            rows[j] = ref[section, :, columns]
+    return jnp.concatenate([rows[j] for j in range(len(rows))], axis=0)
+
+
+def product_tile(x_ref, w_mine, w_other, mine):
     m = x_ref.shape[0] // 2
     by_mine = jnp.dot(x_ref[...], w_mine, preferred_element_type=F32)
     by_other = jnp.dot(x_ref[...], w_other, preferred_element_type=F32)
@@ -88,15 +80,16 @@
     x_in, x_now, y_out = rest
     me, mine = scalars[0], scalars[1]
     for kc, piece in enumerate(pieces):
-        x_in[:, 2 * kc : 2 * kc + 2] = piece[:, :, chunk * rc : (chunk + 1) * rc, :]
+        lo = chunk * rc if piece.shape[2] > rc else 0
+        x_in[:, 2 * kc : 2 * kc + 2] = piece[:, :, lo : lo + rc, :]
     k = x_now.shape[1]
     low_half = lax.broadcasted_iota(jnp.int32, (rc, LANES), 1) < q
     tile = 2 * LANES
 
     def swapped(section, store):
         for lo in range(0, k, tile):
-            halves = branch_tile(places, w_refs, section, mine, pl.ds(lo, tile))
-            for p, y in enumerate(product_tile_halves(x_now, *halves, mine)):
+            halves = [branch_rows(places, w_refs, section, mine, pl.ds(lo, tile), half) for half in (0, 1)]
+            for p, y in enumerate(product_tile(x_now, *halves, mine)):
                 for s in range(0, tile, LANES):
                     part = y[:, s : s + LANES]
                     turned = pltpu.roll(part, q, 1)
@@ -134,18 +127,16 @@
     put.wait()
 
 
-def turn_kernel(places, n_w, scalars, picks, *rest):
-    w_refs, out = rest[:n_w], rest[n_w]
-    mine = scalars[1]
+def turn_kernel(places, half, scalars, picks, *rest):
+    w_refs, out = rest[:-1], rest[-1]
     pick = picks[picks.shape[0] - 1]
-    for lo in range(0, out.shape[2], 2 * LANES):
+    for lo in range(0, out.shape[1], 2 * LANES):
         columns = pl.ds(lo, 2 * LANES)
-        for half, w in enumerate(branch_tile(places, w_refs, 0, mine, columns)):
-            turned = jnp.dot(pick, w, preferred_element_type=F32).astype(BF16)
-            out[mine if half == 0 else 1 - mine, :, columns] = turned
-
-
-def fin_kernel(n, rc, chunk, with_prev, scalars, branch, *rest):
+        w = branch_rows(places, w_refs, 0, scalars[1], columns, half)
+        out[:, columns] = jnp.dot(pick, w, preferred_element_type=F32).astype(BF16)
+
+
+def fin_kernel(n, rc, chunk, with_prev, scalars, w_mine, w_other, *rest):
     pieces, forwarded, rest = rest[: n // 2], rest[n // 2], rest[n // 2 + 1 :]
     if with_prev:
         rest = rest[1:]
@@ -159,7 +150,7 @@
     tile = 2 * LANES
     x_now = x_in.reshape(2 * n * rc, k)
     for lo in range(0, k, tile):
-        for p, y in enumerate(product_tile(x_now, branch[0, :, lo : lo + tile], branch[1, :, lo : lo + tile])):
+        for p, y in enumerate(product_tile(x_now, w_mine[:, lo : lo + tile], w_other[:, lo : lo + tile], scalars[1])):
             y_out[p, :, :, lo : lo + tile] = y.astype(BF16).reshape(n, rc, tile)
     for j in range(n):
         start = pl.multiple_of((me ^ j) * rows + chunk * rc, rc)
@@ -190,7 +181,7 @@
         copy.wait()
 
 
-def pack_kernel(scalars, stem, sib, *rest):
+def pack_kernel(plan, scalars, stem, sib, *rest):
     outs, (x, sems) = rest[:-2], rest[-2:]
     core, chip = scalars[0] & 1, scalars[0] >> 1
     takes = [
@@ -201,9 +192,10 @@
         take.start()
     for take in takes:
         take.wait()
-    for kc in reversed(range(len(outs))):
+    for out, (kc, lo) in zip(outs, plan):
         for cr in range(2):
-            pltpu.make_async_copy(x.at[cr, :, chip ^ kc], outs[kc].at[:, cr], sems.at[2]).start()
+            source = x.at[cr, :, chip ^ kc, pl.ds(lo, out.shape[2])]
+            pltpu.make_async_copy(source, out.at[:, cr], sems.at[2]).start()
     wait_all(x, sems.at[2])
 
 
@@ -280,33 +272,35 @@
     top, low = n // 2, n // 4
     own_sib = swap_inner(branches, 1)
 
+    def own_half(first, count, part):
+        return lax.dynamic_slice(branches, (first, part, 0, 0), (count, 1, q, k))[:, 0]
+
     def start_gather(first, count):
-        mine = lax.dynamic_slice(branches, (first, mine_index, 0, 0), (count, 1, q, k))[:, 0]
+        mine = own_half(first, count, mine_index)
         far = swap_inner(mine, top | low)
         near = swap_inner(mine, low)
         held = {0: (mine, None), low: (near, None), top | low: (far, None)}
         held[top] = (swap_inner(far, low), None)
         return held
 
-    def finish_gather(held, others, groups, first):
+    def finish_gather(groups, first):
         sources, places = [], []
 
-        def place(value, j, half):
+        def place(value, half, j):
             array, item = value
             at = next((i for i, other in enumerate(sources) if other is array), len(sources))
             sources[at:] = [array] if at == len(sources) else sources[at:]
-            places.append((at, item, half, j))
+            places.append((at, item, half, j, 0))
 
         for group in groups:
-            parts = [(held[i], 0, i) for i in group] + [(others[i], 1, i) for i in group]
-            got = swap_inner(joined([part[0] for part in parts]), 1)
-            for at, (value, half, i) in enumerate(parts):
-                place(value, i, half)
-                place((got, at), i + 1, half)
-        places += [(len(sources), None, None, 0), (len(sources) + 1, None, None, 1)]
-        sources += [branches, own_sib]
-        shifted = [(at, item, half, j, first if half is None else 0) for at, item, half, j in places]
-        return sources, tuple(shifted)
+            got = swap_inner(joined([value for value, _, _ in group]), 1)
+            for at, (value, half, i) in enumerate(group):
+                place(value, half, i)
+                place((got, at), half, i + 1)
+        for j, array in enumerate((branches, own_sib)):
+            places.append((len(sources), None, None, j, first))
+            sources.append(array)
+        return sources, tuple(places)
 
     def gather_by_piece(first, count):
         held = start_gather(first, count)
@@ -315,10 +309,16 @@
             for i in list(held):
                 held[i | bit] = (swap_inner(held[i][0], bit), None)
             bit //= 2
-        others = {i: (swap_parts(held[i][0]), None) for i in held if i}
-        last = [i for i in held if i & 2 and i & top]
-        early = [i for i in held if i and i not in last]
-        return finish_gather(held, others, [early, last], first)
+        other = own_half(first, count, 1 - mine_index)
+        others = {i: (swap_inner(other, i), None) for i in (low, 2)}
+        rest = [i for i in held if i]
+        for i in rest:
+            if i not in others:
+                others[i] = (swap_parts(held[i][0]), None)
+        last = [i for i in rest if i & 2 and i & top]
+        early = [i for i in rest if i not in last]
+        groups = [[(held[i], 0, i) for i in part] + [(others[i], 1, i) for i in part] for part in (early, last)]
+        return finish_gather(groups, first)
 
     def gather_joined(first, count):
         held = start_gather(first, count)
@@ -330,8 +330,8 @@
             bit //= 2
         rest = [i for i in held if i]
         got = swap_parts(joined([held[i] for i in rest]))
-        others = {i: (got, at) for at, i in enumerate(rest)}
-        return finish_gather(held, others, [rest], first)
+        groups = [[(held[i], 0, i) for i in rest], [((got, at), 1, i) for at, i in enumerate(rest)]]
+        return finish_gather(groups, first)
 
     def chip_exchange(payloads):
         got = [payloads[0]] + [None] * (chips - 1)
@@ -354,17 +354,23 @@
     )(scalars, column_order.reshape(sections, k // LANES, LANES))
 
     from_sib = swap_inner(for_sib, 1)
+    plan = [(kc, chunk * rc, rc) for kc in range(chips) for chunk in range(CHUNKS)]
     payloads = pl.pallas_call(
-        pack_kernel,
-        out_shape=[shape(2, 2, block, k)] * chips,
+        functools.partial(pack_kernel, tuple(entry[:2] for entry in plan)),
+        out_shape=[shape(2, 2, size, k) for _, _, size in plan],
         in_specs=[smem, ANY, ANY],
-        out_specs=[ANY] * chips,
+        out_specs=[ANY] * len(plan),
         scratch_shapes=[vmem((2, 2, chips, block, k), BF16), pltpu.SemaphoreType.DMA((3,))],
         cost_estimate=flat_cost(0, 8 * rows * k),
         compiler_params=ROOM,
         name="pack",
     )(scalars, by_core, from_sib)
-    pieces = chip_exchange(payloads)
+    pieces = [[None] * chips for _ in range(CHUNKS)]
+    for payload, (kc, lo, size) in zip(payloads, plan):
+        chunk = lo // rc
+        got = swap_inner(payload, 2 * kc) if kc else payload
+        for number in range(chunk, chunk + size // rc):
+            pieces[number][kc] = got
 
     mm = 8 * m * k * k
 
@@ -381,21 +387,26 @@
             ],
             cost_estimate=flat_cost(3 * mm, 16 * k * k),
             compiler_params=ROOM,
-        )(scalars, picks, *pieces, *a_stacks)
-
-    branch = pl.pallas_call(
-        functools.partial(turn_kernel, b_places, len(b_stacks)),
-        out_shape=shape(2, k, k),
-        in_specs=[smem] + [VMEM] * (1 + len(b_stacks)),
-        out_specs=VMEM,
-        cost_estimate=flat_cost(4 * k * k * k, 8 * k * k),
-        compiler_params=ROOM,
-        name="turn",
-    )(scalars, picks, *b_stacks)
+        )(scalars, picks, *pieces[chunk], *a_stacks)
+
+    def turn(half):
+        used = [place for place in b_places if place[2] in (None, half)]
+        numbers = sorted({place[0] for place in used})
+        used = tuple((numbers.index(place[0]),) + place[1:] for place in used)
+        return pl.pallas_call(
+            functools.partial(turn_kernel, used, half),
+            out_shape=shape(k, k),
+            in_specs=[smem] + [VMEM] * (1 + len(numbers)),
+            out_specs=VMEM,
+            cost_estimate=flat_cost(2 * k * k * k, 4 * k * k),
+            compiler_params=ROOM,
+        )(scalars, picks, *[b_stacks[at] for at in numbers])
+
+    turned = [turn(0), turn(1)]
 
     def fin(chunk, arrived, prev):
         extra = [] if prev is None else [prev]
-        n_in = 3 + chips
+        n_in = 4 + chips
         return pl.pallas_call(
             functools.partial(fin_kernel, n, rc, chunk, bool(extra)),
             out_shape=shape(2, rows, k),
@@ -409,7 +420,7 @@
             input_output_aliases={n_in: 0} if extra else {},
             cost_estimate=flat_cost(mm, 8 * k * k),
             compiler_params=ROOM,
-        )(scalars, branch, *arrived, *extra)
+        )(scalars, *turned, *arrived, *extra)
 
     result = None
     for chunk in range(CHUNKS):

time: 246 us -> 211 us (0.86)
  waiting for transfers between devices: 121 us -> 98 us
  starting transfers between devices: 76.1 us -> 63.3 us
    ppermute x8 -> x6, waiting for transfers between devices: 26.6 us -> 8.51 us  [swap_parts(): return lax.ppermute(x, 'parts', [(i, i ^ 1) for i in range(n_parts)])]
    ppermute x39 -> x49, starting transfers between devices: 68.6 us -> 57.4 us  [swap_inner(): return lax.ppermute(x, 'inner', [(i, i ^ mask) for i in range(n)])]
    ppermute x39 -> x49, waiting for transfers between devices: 94.6 us -> 89.5 us  [swap_inner(): return lax.ppermute(x, 'inner', [(i, i ^ mask) for i in range(n)])]
    ppermute x8 -> x6, starting transfers between devices: 7.49 us -> 5.96 us  [swap_parts(): return lax.ppermute(x, 'parts', [(i, i ^ 1) for i in range(n_parts)])]
    pallas_call x2 -> x3, Pallas kernels: 7.48 us -> 7.86 us  [the longest x2 5.74 us: turn(): pl.pallas_call(functools.partial(turn_kernel, used, half), out_shape=shap...]
  transfers between devices with their start and end apart: 47 -> 55, of which waited for: 25 -> 28; matrix products, arithmetic and copies ran while one was open for 0% -> 0% of each run, Pallas kernels for 16% -> 19%
where the time goes in v2:
time: 211 us; the launch traced here: 209 us
  waiting for transfers between devices  98 us (46%)
  starting transfers between devices  63.3 us (30%)
  Pallas kernels  46.3 us (22%)
    ppermute x49, waiting for transfers between devices, swap_inner(): return lax.ppermute(x, 'inner', [(i, i ^ mask) for i in range(n)])  89.5 us
    ppermute x49, starting transfers between devices, swap_inner(): return lax.ppermute(x, 'inner', [(i, i ^ mask) for i in range(n)])  57.4 us
    pallas_call x2, Pallas kernels, mid(): pl.pallas_call(functools.partial(mid_kernel, n, q, rc, chunk, a_places, l...  18 us
    ppermute x6, waiting for transfers between devices, swap_parts(): return lax.ppermute(x, 'parts', [(i, i ^ 1) for i in range(n_parts)])  8.51 us
    pallas_call x2, Pallas kernels, fin(): pl.pallas_call(functools.partial(fin_kernel, n, rc, chunk, bool(extra)),...  7.78 us
    pallas_call x5, Pallas kernels, joined(): pl.pallas_call(functools.partial(join_kernel, tuple(items)), out_shape=wh...  7.34 us
    ppermute x6, starting transfers between devices, swap_parts(): return lax.ppermute(x, 'parts', [(i, i ^ 1) for i in range(n_parts)])  5.96 us
    pallas_call x2, Pallas kernels, turn(): pl.pallas_call(functools.partial(turn_kernel, used, half), out_shape=shap...  5.74 us
  transfers between devices with their start and end apart: 55, of which 28 were waited for; matrix products, arithmetic and copies ran while one was open for 0% of the time, Pallas kernels for 19%

profile of v2, /device:TPU:13, one launch (start us, length us, event | category | flops | bytes accessed | tf_op | source)
XLA Modules:
  0.0 209.5 jit_solution(8177601793760177423)
XLA Ops:
  1.1 1.4 collective-permute-start.17
  2.4 2.2 %collective-permute-start.16 = (bf16[2,64,1024]{2,1,0:T(8,128)(2,1)S(1)}, bf16[2,64,1024]{2,1,0:T(8,128)(2,1)S(1)}, u32[]{:S(2)}, u32[]{:S(2)}) collective-permute-start(bf16[2,64,1024]{2,1,0:T(8,128)(2,1)S(1)} %get-tuple-element.70), channel_id=1, source_target_pairs={{0,4},{1,5},{2,6},{3,7},{4,0},{5,1},{6,2},{7,3},{8,12},{9,13},{10,... | collective-permute-start | bytes 786440 | tf_op jit(solution)/shard_map/ppermute | solution.py:229
  4.9 9.3 %collective-permute-done.17.refs_1_.rest_10_ = bf16[2,64,1024]{2,1,0:T(8,128)(2,1)S(1)} collective-permute-done((bf16[2,64,1024]{2,1,0:T(8,128)(2,1)S(1)}, bf16[2,64,1024]{2,1,0:T(8,128)(2,1)S(1)}, u32[]{:S(2)}, u32[]{:S(2)}) %collective-permute-start.17) | collective-permute-done | bytes 262176 | tf_op jit(solution)/shard_map/ppermute | solution.py:229
  14.1 1.9 collective-permute-done.16.refs_0_.rest_8_
  17.3 1.2 collective-permute-start.19
  18.6 1.2 collective-permute-start.22
  19.8 1.6 collective-permute-done.18.refs_2_.rest_11_
  21.4 1.2 collective-permute-start.23
  23.5 3.4 %collective-permute-done.21.refs_5_.rest_14_ = bf16[2,64,1024]{2,1,0:T(8,128)(2,1)S(1)} collective-permute-done((bf16[2,64,1024]{2,1,0:T(8,128)(2,1)S(1)}, bf16[2,64,1024]{2,1,0:T(8,128)(2,1)S(1)}, u32[]{:S(2)}, u32[]{:S(2)}) %collective-permute-start.21) | collective-permute-done | bytes 262176 | tf_op jit(solution)/shard_map/ppermute | solution.py:229
  27.8 2.9 %collective-permute-done.23.refs_7_.rest_16_ = bf16[2,64,1024]{2,1,0:T(8,128)(2,1)S(1)} collective-permute-done((bf16[2,64,1024]{2,1,0:T(8,128)(2,1)}, bf16[2,64,1024]{2,1,0:T(8,128)(2,1)S(1)}, u32[]{:S(2)}, u32[]{:S(2)}) %collective-permute-start.23) | collective-permute-done | bytes 262176 | tf_op jit(solution)/shard_map/ppermute | solution.py:232
  30.6 5.6 %collective-permute-done.25.refs_9_.rest_18_ = bf16[2,64,1024]{2,1,0:T(8,128)(2,1)S(1)} collective-permute-done((bf16[2,64,1024]{2,1,0:T(8,128)(2,1)S(1)}, bf16[2,64,1024]{2,1,0:T(8,128)(2,1)S(1)}, u32[]{:S(2)}, u32[]{:S(2)}) %collective-permute-start.25) | collective-permute-done | bytes 262176 | tf_op jit(solution)/shard_map/ppermute | solution.py:232
  36.3 2.6 %shard_map.42 = bf16[10,2,64,1024]{3,2,1,0:T(8,128)(2,1)} custom-call(bf16[2,64,1024]{2,1,0:T(8,128)(2,1)S(1)} %collective-permute-done.16.refs_0_.rest_8_, bf16[2,64,1024]{2,1,0:T(8,128)(2,1)S(1)} %collective-permute-done.17.refs_1_.rest_10_, bf16[2,64,1024]{2,1,0:T(8,128)(2,1)} %collective-permute-done.18.refs_2_.rest_11_, ...), custom_call_target="tpu_custom_call" | custom-call | bytes 5242880 | tf_op jit(solution)/shard_map/pallas_call | solution.py:262
  38.9 2.3 %collective-permute-start.26 = (bf16[10,2,64,1024]{3,2,1,0:T(8,128)(2,1)}, bf16[10,2,64,1024]{3,2,1,0:T(8,128)(2,1)}, u32[]{:S(2)}, u32[]{:S(2)}) collective-permute-start(bf16[10,2,64,1024]{3,2,1,0:T(8,128)(2,1)} %shard_map.42), channel_id=1, source_target_pairs={{0,1},{1,0},{2,3},{3,2},{4,5},{5,4},{6,7},{7,6},{8,9},{9,8},{10,11... | collective-permute-start | bytes 7864328 | tf_op jit(solution)/shard_map/ppermute | solution.py:229
  41.5 1.2 collective-permute-start.28
  44.2 4.9 %collective-permute-done.27.refs_0_.rest_19_ = bf16[2,64,1024]{2,1,0:T(8,128)(2,1)} collective-permute-done((bf16[2,64,1024]{2,1,0:T(8,128)(2,1)S(1)}, bf16[2,64,1024]{2,1,0:T(8,128)(2,1)}, u32[]{:S(2)}, u32[]{:S(2)}) %collective-permute-start.27) | collective-permute-done | bytes 262176 | tf_op jit(solution)/shard_map/ppermute | solution.py:229
  49.2 1.2 collective-permute-start.29
  50.4 4.4 %collective-permute-done.28.refs_1_.rest_21_ = bf16[2,64,1024]{2,1,0:T(8,128)(2,1)} collective-permute-done((bf16[2,64,1024]{2,1,0:T(8,128)(2,1)}, bf16[2,64,1024]{2,1,0:T(8,128)(2,1)}, u32[]{:S(2)}, u32[]{:S(2)}) %collective-permute-start.28) | collective-permute-done | bytes 262176 | tf_op jit(solution)/shard_map/ppermute | solution.py:229
  54.8 1.2 collective-permute-start.30
  56.1 7.0 %collective-permute-done.1.refs_2_.refs_1_.rest_2_ = bf16[1,64,1024]{2,1,0:T(8,128)(2,1)S(1)} collective-permute-done((bf16[1,64,1024]{2,1,0:T(8,128)(2,1)S(1)}, bf16[1,64,1024]{2,1,0:T(8,128)(2,1)S(1)}, u32[]{:S(2)}, u32[]{:S(2)}) %collective-permute-start.1) | collective-permute-done | bytes 131104 | tf_op jit(solution)/shard_map/ppermute | solution.py:229
  63.1 1.7 collective-permute-start.5
  64.8 1.5 collective-permute-start.2
  66.3 1.1 shard_map.43
  67.4 2.5 %collective-permute-done.refs_1_.refs_0_.rest_0_ = bf16[1,64,1024]{2,1,0:T(8,128)(2,1)S(1)} collective-permute-done((bf16[1,64,1024]{2,1,0:T(8,128)(2,1)S(1)}, bf16[1,64,1024]{2,1,0:T(8,128)(2,1)S(1)}, u32[]{:S(2)}, u32[]{:S(2)}) %collective-permute-start) | collective-permute-done | bytes 131104 | tf_op jit(solution)/shard_map/ppermute | solution.py:229
  69.8 1.3 collective-permute-start.31
  71.2 1.5 collective-permute-done.2.refs_3_.refs_2_.rest_3_
  73.7 2.1 %pack.1 = (bf16[2,2,16,1024]{3,2,1,0:T(8,128)(2,1)S(1)}, bf16[2,2,16,1024]{3,2,1,0:T(8,128)(2,1)S(1)}, bf16[2,2,16,1024]{3,2,1,0:T(8,128)(2,1)S(1)}, bf16[2,2,16...) custom-call(s32[2]{0:T(128)S(1)} %pad_add_fusion.scalars, ...), custom_call_target="tpu_custom_call" | custom-call | bytes 4194304 | tf_op jit(solution)/shard_map/pack/pallas_call | solution.py:358
  75.8 1.3 collective-permute-start.9
  77.1 9.0 %collective-permute-done.3.refs_3_.rest_4_ = bf16[4,1,64,1024]{3,2,1,0:T(8,128)(2,1)S(1)} collective-permute-done((bf16[4,1,64,1024]{3,2,1,0:T(8,128)(2,1)S(1)}, bf16[4,1,64,1024]{3,2,1,0:T(8,128)(2,1)S(1)}, u32[]{:S(2)}, u32[]{:S(2)}) %collective-permute-start.3) | collective-permute-done | bytes 524320 | tf_op jit(solution)/shard_map/ppermute | solution.py:229
  86.6 2.3 %collective-permute-done.9.rest_1_ = bf16[2,2,16,1024]{3,2,1,0:T(8,128)(2,1)S(1)} collective-permute-done((bf16[2,2,16,1024]{3,2,1,0:T(8,128)(2,1)S(1)}, bf16[2,2,16,1024]{3,2,1,0:T(8,128)(2,1)S(1)}, u32[]{:S(2)}, u32[]{:S(2)}) %collective-permute-start.9) | collective-permute-done | bytes 131104 | tf_op jit(solution)/shard_map/ppermute | solution.py:229
  89.1 1.4 shard_map.38
  91.8 2.1 collective-permute-done.42.rest_3_
  94.5 3.0 %collective-permute-done.43.rest_4_ = bf16[2,2,16,1024]{3,2,1,0:T(8,128)(2,1)S(1)} collective-permute-done((bf16[2,2,16,1024]{3,2,1,0:T(8,128)(2,1)S(1)}, bf16[2,2,16,1024]{3,2,1,0:T(8,128)(2,1)S(1)}, u32[]{:S(2)}, u32[]{:S(2)}) %collective-permute-start.43) | collective-permute-done | bytes 131104 | tf_op jit(solution)/shard_map/ppermute | solution.py:229
  97.7 5.0 %collective-permute-done.44.rest_5_ = bf16[2,2,16,1024]{3,2,1,0:T(8,128)(2,1)S(1)} collective-permute-done((bf16[2,2,16,1024]{3,2,1,0:T(8,128)(2,1)S(1)}, bf16[2,2,16,1024]{3,2,1,0:T(8,128)(2,1)S(1)}, u32[]{:S(2)}, u32[]{:S(2)}) %collective-permute-start.44) | collective-permute-done | bytes 131104 | tf_op jit(solution)/shard_map/ppermute | solution.py:229
  102.7 1.5 collective-permute-start.46
  104.3 3.0 %picks.1 = bf16[3,1024,1024]{2,1,0:T(8,128)(2,1)S(1)} custom-call(s32[2]{0:T(128)S(1)} %pad_add_fusion.scalars, s32[3,8,128]{2,1,0:T(8,128)S(1)} %bitcast.15), custom_call_target="tpu_custom_call" | custom-call | bytes 6291456 | tf_op jit(solution)/shard_map/picks/pallas_call | solution.py:345
  107.3 1.3 collective-permute-done.45.rest_6_
  108.5 2.3 %collective-permute-start.10 = (bf16[2,2,16,1024]{3,2,1,0:T(8,128)(2,1)S(1)}, bf16[2,2,16,1024]{3,2,1,0:T(8,128)(2,1)S(1)}, u32[]{:S(2)}, u32[]{:S(2)}) collective-permute-start(bf16[2,2,16,1024]{3,2,1,0:T(8,128)(2,1)S(1)} %get-tuple-element.39), channel_id=1, source_target_pairs={{0,4},{1,5},{2,6},{3,7},{4,0},{5,1},{6,2},{7,3},{8,12},{9,13},{10,... | collective-permute-start | bytes 393224 | tf_op jit(solution)/shard_map/ppermute | solution.py:229
  110.9 3.7 %collective-permute-done.46.rest_7_ = bf16[2,2,16,1024]{3,2,1,0:T(8,128)(2,1)S(1)} collective-permute-done((bf16[2,2,16,1024]{3,2,1,0:T(8,128)(2,1)S(1)}, bf16[2,2,16,1024]{3,2,1,0:T(8,128)(2,1)S(1)}, u32[]{:S(2)}, u32[]{:S(2)}) %collective-permute-start.46) | collective-permute-done | bytes 131104 | tf_op jit(solution)/shard_map/ppermute | solution.py:229
  115.2 2.9 %collective-permute-start.13 = (bf16[2,2,16,1024]{3,2,1,0:T(8,128)(2,1)S(1)}, bf16[2,2,16,1024]{3,2,1,0:T(8,128)(2,1)S(1)}, u32[]{:S(2)}, u32[]{:S(2)}) collective-permute-start(bf16[2,2,16,1024]{3,2,1,0:T(8,128)(2,1)S(1)} %get-tuple-element.42), channel_id=1, source_target_pairs={{0,10},{1,11},{2,8},{3,9},{4,14},{5,15},{6,12},{7,13},{8,2},{9,3},... | collective-permute-start | bytes 393224 | tf_op jit(solution)/shard_map/ppermute | solution.py:229
  118.2 9.0 %shard_map.46 = (bf16[2,2,16,1024]{3,2,1,0:T(8,128)(2,1)S(1)}, bf16[2,2,16,1024]{3,2,1,0:T(8,128)(2,1)S(1)}, bf16[2,2,16,1024]{3,2,1,0:T(8,128)(2,1)S(1)}, bf16[...) custom-call(s32[2]{0:T(128)S(1)} %pad_add_fusion.scalars, ...), custom_call_target="tpu_custom_call" | custom-call | flops 6442450944 | bytes 16777216 | tf_op jit(solution)/shard_map/pallas_call | solution.py:378
  127.4 1.5 collective-permute-start.15
  130.0 3.0 %collective-permute-start.48 = (bf16[2,2,16,1024]{3,2,1,0:T(8,128)(2,1)S(1)}, bf16[2,2,16,1024]{3,2,1,0:T(8,128)(2,1)S(1)}, u32[]{:S(2)}, u32[]{:S(2)}) collective-permute-start(bf16[2,2,16,1024]{3,2,1,0:T(8,128)(2,1)S(1)} %get-tuple-element.63), channel_id=1, source_target_pairs={{0,4},{1,5},{2,6},{3,7},{4,0},{5,1},{6,2},{7,3},{8,12},{9,13},{10,... | collective-permute-start | bytes 393224 | tf_op jit(solution)/shard_map/ppermute | solution.py:229
  133.2 1.6 shard_map.40
  134.8 5.7 %collective-permute-start.4 = (bf16[7,1,64,1024]{3,2,1,0:T(8,128)(2,1)S(1)}, bf16[7,1,64,1024]{3,2,1,0:T(8,128)(2,1)S(1)}, u32[]{:S(2)}, u32[]{:S(2)}) collective-permute-start(bf16[7,1,64,1024]{3,2,1,0:T(8,128)(2,1)S(1)} %shard_map.38), channel_id=1, source_target_pairs={{0,1},{1,0},{2,3},{3,2},{4,5},{5,4},{6,7},{7,6},{8,9},{9,8},{10,11... | collective-permute-start | bytes 2752520 | tf_op jit(solution)/shard_map/ppermute | solution.py:229
  140.5 1.9 collective-permute-start.7
  142.4 1.2 collective-permute-start.50
  143.5 1.4 collective-permute-start.51
  145.6 9.0 %shard_map.44 = (bf16[2,2,16,1024]{3,2,1,0:T(8,128)(2,1)S(1)}, bf16[2,2,16,1024]{3,2,1,0:T(8,128)(2,1)S(1)}, bf16[2,2,16,1024]{3,2,1,0:T(8,128)(2,1)S(1)}, bf16[...) custom-call(s32[2]{0:T(128)S(1)} %pad_add_fusion.scalars, ...), custom_call_target="tpu_custom_call" | custom-call | flops 6442450944 | bytes 16777216 | tf_op jit(solution)/shard_map/pallas_call | solution.py:378
  154.6 1.6 collective-permute-start.53
  157.0 1.3 collective-permute-start.32
  158.3 1.6 collective-permute-done.52.refs_6_.rest_6_
  159.8 7.2 %collective-permute-done.53.refs_7_.rest_7_ = bf16[2,2,16,1024]{3,2,1,0:T(8,128)(2,1)S(1)} collective-permute-done((bf16[2,2,16,1024]{3,2,1,0:T(8,128)(2,1)S(1)}, bf16[2,2,16,1024]{3,2,1,0:T(8,128)(2,1)S(1)}, u32[]{:S(2)}, u32[]{:S(2)}) %collective-permute-start.53) | collective-permute-done | bytes 131104 | tf_op jit(solution)/shard_map/ppermute | solution.py:229
  167.0 2.7 %collective-permute-start.35 = (bf16[2,2,16,1024]{3,2,1,0:T(8,128)(2,1)S(1)}, bf16[2,2,16,1024]{3,2,1,0:T(8,128)(2,1)S(1)}, u32[]{:S(2)}, u32[]{:S(2)}) collective-permute-start(bf16[2,2,16,1024]{3,2,1,0:T(8,128)(2,1)S(1)} %get-tuple-element.49), channel_id=1, source_target_pairs={{0,8},{1,9},{2,10},{3,11},{4,12},{5,13},{6,14},{7,15},{8,0},{9,1},... | collective-permute-start | bytes 393224 | tf_op jit(solution)/shard_map/ppermute | solution.py:229
  170.8 1.5 collective-permute-done.34.refs_3_.rest_3_
  172.2 1.5 collective-permute-start.37
  173.8 1.9 collective-permute-done.35.refs_4_.rest_4_
  176.7 6.6 %collective-permute-done.36.refs_5_.rest_5_ = bf16[2,2,16,1024]{3,2,1,0:T(8,128)(2,1)S(1)} collective-permute-done((bf16[2,2,16,1024]{3,2,1,0:T(8,128)(2,1)S(1)}, bf16[2,2,16,1024]{3,2,1,0:T(8,128)(2,1)S(1)}, u32[]{:S(2)}, u32[]{:S(2)}) %collective-permute-start.36) | collective-permute-done | bytes 131104 | tf_op jit(solution)/shard_map/ppermute | solution.py:229
  183.4 2.2 %collective-permute-start.54 = (bf16[8,2,16,1024]{3,2,1,0:T(8,128)(2,1)S(1)}, bf16[8,2,16,1024]{3,2,1,0:T(8,128)(2,1)S(1)}, u32[]{:S(2)}, u32[]{:S(2)}) collective-permute-start(bf16[8,2,16,1024]{3,2,1,0:T(8,128)(2,1)S(1)} %shard_map.47), channel_id=1, source_target_pairs={{0,1},{1,0},{2,3},{3,2},{4,5},{5,4},{6,7},{7,6},{8,9},{9,8},{10,11... | collective-permute-start | bytes 1572872 | tf_op jit(solution)/shard_map/ppermute | solution.py:229
  186.4 4.4 %collective-permute-done.38.refs_7_.rest_7_ = bf16[2,2,16,1024]{3,2,1,0:T(8,128)(2,1)S(1)} collective-permute-done((bf16[2,2,16,1024]{3,2,1,0:T(8,128)(2,1)S(1)}, bf16[2,2,16,1024]{3,2,1,0:T(8,128)(2,1)S(1)}, u32[]{:S(2)}, u32[]{:S(2)}) %collective-permute-start.38) | collective-permute-done | bytes 131104 | tf_op jit(solution)/shard_map/ppermute | solution.py:229
  191.7 4.0 %collective-permute-start.39 = (bf16[8,2,16,1024]{3,2,1,0:T(8,128)(2,1)S(1)}, bf16[8,2,16,1024]{3,2,1,0:T(8,128)(2,1)S(1)}, u32[]{:S(2)}, u32[]{:S(2)}) collective-permute-start(bf16[8,2,16,1024]{3,2,1,0:T(8,128)(2,1)S(1)} %shard_map.45), channel_id=1, source_target_pairs={{0,1},{1,0},{2,3},{3,2},{4,5},{5,4},{6,7},{7,6},{8,9},{9,8},{10,11... | collective-permute-start | bytes 1572872 | tf_op jit(solution)/shard_map/ppermute | solution.py:229
  195.7 2.9 %shard_map.39.w_mine = bf16[1024,1024]{1,0:T(8,128)(2,1)S(1)} custom-call(s32[2]{0:T(128)S(1)} %pad_add_fusion.scalars, bf16[3,1024,1024]{2,1,0:T(8,128)(2,1)S(1)} %picks.1, bf16[1,64,1024]{2,1,0:T(8,128)(2,1)S(1)} %collective-permute-done.refs_1_.refs_0_.rest_0_, bf16[7,1,64,1024]{3,2,1,0:T(8,128)(2,1)S(1)} %collective-permute-done.4.rest_1_, ...), custom_call_target="tpu_custom_call" | custom-call | flops 2147483648 | bytes 4194304 | tf_op jit(solution)/shard_map/pallas_call | solution.py:396
  198.6 2.9 %shard_map.41.w_other = bf16[1024,1024]{1,0:T(8,128)(2,1)S(1)} custom-call(s32[2]{0:T(128)S(1)} %pad_add_fusion.scalars, bf16[3,1024,1024]{2,1,0:T(8,128)(2,1)S(1)} %picks.1, bf16[7,1,64,1024]{3,2,1,0:T(8,128)(2,1)S(1)} %collective-permute-done.6.refs_0_.rest_0_, bf16[7,1,64,1024]{3,2,1,0:T(8,128)(2,1)S(1)} %collective-permute-done.7.rest_1_, ...), custom_call_target="tpu_custom_call" | custom-call | flops 2147483648 | bytes 4194304 | tf_op jit(solution)/shard_map/pallas_call | solution.py:396
  201.5 3.9 %shard_map.48.rest_9_ = bf16[2,512,1024]{2,1,0:T(8,128)(2,1)} custom-call(s32[2]{0:T(128)S(1)} %pad_add_fusion.scalars, bf16[1024,1024]{1,0:T(8,128)(2,1)S(1)} %shard_map.39.w_mine, bf16[1024,1024]{1,0:T(8,128)(2,1)S(1)} %shard_map.41.w_other, bf16[2,2,16,1024]{3,2,1,0:T(8,128)(2,1)S(1)} %get-tuple-element.61.refs_0_.rest_0_, ...), custom_call_target="tpu_custom_call" | custom-call | flops 2147483648 | bytes 8388608 | tf_op jit(solution)/shard_map/pallas_call | solution.py:410
  205.4 3.9 %shard_map.49 = bf16[2,512,1024]{2,1,0:T(8,128)(2,1)} custom-call(s32[2]{0:T(128)S(1)} %pad_add_fusion.scalars, bf16[1024,1024]{1,0:T(8,128)(2,1)S(1)} %shard_map.39.w_mine, bf16[1024,1024]{1,0:T(8,128)(2,1)S(1)} %shard_map.41.w_other, bf16[2,2,16,1024]{3,2,1,0:T(8,128)(2,1)S(1)} %get-tuple-element.45.refs_0_.rest_0_, ...), custom_call_target="tpu_custom_call", output_to_operand_aliasing={{}: (12, {})} | custom-call | flops 2147483648 | bytes 8388608 | tf_op jit(solution)/shard_map/pallas_call | solution.py:410
  (100 shorter events, 17.3 us)
Async XLA Ops:
  1.1 13.1 %collective-permute-start.17 = (bf16[2,64,1024]{2,1,0:T(8,128)(2,1)S(1)}, bf16[2,64,1024]{2,1,0:T(8,128)(2,1)S(1)}, u32[]{:S(2)}, u32[]{:S(2)}) collective-permute-start(bf16[2,64,1024]{2,1,0:T(8,128)(2,1)S(1)} %get-tuple-element.70), channel_id=1, source_target_pairs={{0,12},{1,13},{2,14},{3,15},{4,8},{5,9},{6,10},{7,11},{8,4},{9,5},... | collective-permute-start | bytes 786440 | tf_op jit(solution)/shard_map/ppermute | solution.py:229
  2.4 13.6 %collective-permute-start.16 = (bf16[2,64,1024]{2,1,0:T(8,128)(2,1)S(1)}, bf16[2,64,1024]{2,1,0:T(8,128)(2,1)S(1)}, u32[]{:S(2)}, u32[]{:S(2)}) collective-permute-start(bf16[2,64,1024]{2,1,0:T(8,128)(2,1)S(1)} %get-tuple-element.70), channel_id=1, source_target_pairs={{0,4},{1,5},{2,6},{3,7},{4,0},{5,1},{6,2},{7,3},{8,12},{9,13},{10,... | collective-permute-start | bytes 786440 | tf_op jit(solution)/shard_map/ppermute | solution.py:229
  4.6 38.2 %copy-start = (bf16[2,512,1024]{2,1,0:T(8,128)(2,1)S(1)}, bf16[2,512,1024]{2,1,0:T(8,128)(2,1)}, u32[]{:S(2)}) copy-start(bf16[2,512,1024]{2,1,0:T(8,128)(2,1)} %param.3) | copy-start | bytes 6291460
  4.6 14.0 %collective-permute-start.24 = (bf16[2,64,1024]{2,1,0:T(8,128)(2,1)S(1)}, bf16[2,64,1024]{2,1,0:T(8,128)(2,1)S(1)}, u32[]{:S(2)}, u32[]{:S(2)}) collective-permute-start(bf16[2,64,1024]{2,1,0:T(8,128)(2,1)S(1)} %get-tuple-element.69), channel_id=1, source_target_pairs={{0,2},{1,3},{2,0},{3,1},{4,6},{5,7},{6,4},{7,5},{8,10},{9,11},{10,... | collective-permute-start | bytes 786440 | tf_op jit(solution)/shard_map/ppermute | solution.py:229
  14.1 7.2 %collective-permute-start.18 = (bf16[2,64,1024]{2,1,0:T(8,128)(2,1)S(1)}, bf16[2,64,1024]{2,1,0:T(8,128)(2,1)}, u32[]{:S(2)}, u32[]{:S(2)}) collective-permute-start(bf16[2,64,1024]{2,1,0:T(8,128)(2,1)S(1)} %collective-permute-done.17.refs_1_.rest_10_), channel_id=1, source_target_pairs={{0,4},{1,5},{2,6},{3,7},{4,0},{5,1},{6,2},{7,3},{8,12},{9,13},{10,... | collective-permute-start | bytes 786440 | tf_op jit(solution)/shard_map/ppermute | solution.py:229
  16.1 6.5 %collective-permute-start.20 = (bf16[2,64,1024]{2,1,0:T(8,128)(2,1)S(1)}, bf16[2,64,1024]{2,1,0:T(8,128)(2,1)S(1)}, u32[]{:S(2)}, u32[]{:S(2)}) collective-permute-start(bf16[2,64,1024]{2,1,0:T(8,128)(2,1)S(1)} %collective-permute-done.16.refs_0_.rest_8_), channel_id=1, source_target_pairs={{0,2},{1,3},{2,0},{3,1},{4,6},{5,7},{6,4},{7,5},{8,10},{9,11},{10,... | collective-permute-start | bytes 786440 | tf_op jit(solution)/shard_map/ppermute | solution.py:229
  16.3 10.6 %collective-permute-start.21 = (bf16[2,64,1024]{2,1,0:T(8,128)(2,1)S(1)}, bf16[2,64,1024]{2,1,0:T(8,128)(2,1)S(1)}, u32[]{:S(2)}, u32[]{:S(2)}) collective-permute-start(bf16[2,64,1024]{2,1,0:T(8,128)(2,1)S(1)} %get-tuple-element.69), channel_id=1, source_target_pairs={{0,4},{1,5},{2,6},{3,7},{4,0},{5,1},{6,2},{7,3},{8,12},{9,13},{10,... | collective-permute-start | bytes 786440 | tf_op jit(solution)/shard_map/ppermute | solution.py:229
  17.3 10.4 %collective-permute-start.19 = (bf16[2,64,1024]{2,1,0:T(8,128)(2,1)S(1)}, bf16[2,64,1024]{2,1,0:T(8,128)(2,1)S(1)}, u32[]{:S(2)}, u32[]{:S(2)}) collective-permute-start(bf16[2,64,1024]{2,1,0:T(8,128)(2,1)S(1)} %get-tuple-element.70), channel_id=1, source_target_pairs={{0,2},{1,3},{2,0},{3,1},{4,6},{5,7},{6,4},{7,5},{8,10},{9,11},{10,... | collective-permute-start | bytes 786440 | tf_op jit(solution)/shard_map/ppermute | solution.py:229
  18.6 20.3 %copy-start.2 = (bf16[2,64,1024]{2,1,0:T(8,128)(2,1)}, bf16[2,64,1024]{2,1,0:T(8,128)(2,1)S(1)}, u32[]{:S(2)}) copy-start(bf16[2,64,1024]{2,1,0:T(8,128)(2,1)S(1)} %collective-permute-done.24.refs_8_.rest_17_) | copy-start | bytes 786436
  18.6 9.2 %collective-permute-start.22 = (bf16[2,64,1024]{2,1,0:T(8,128)(2,1)S(1)}, bf16[2,64,1024]{2,1,0:T(8,128)(2,1)S(1)}, u32[]{:S(2)}, u32[]{:S(2)}) collective-permute-start(bf16[2,64,1024]{2,1,0:T(8,128)(2,1)S(1)} %collective-permute-done.17.refs_1_.rest_10_), channel_id=1, source_target_pairs={{0,16},{16,0},{1,17},{17,1},{2,18},{18,2},{3,19},{19,3},{4,20},{20... | collective-permute-start | bytes 786440 | tf_op jit(solution)/shard_map/ppermute | solution.py:232
  21.4 9.3 %collective-permute-start.23 = (bf16[2,64,1024]{2,1,0:T(8,128)(2,1)}, bf16[2,64,1024]{2,1,0:T(8,128)(2,1)S(1)}, u32[]{:S(2)}, u32[]{:S(2)}) collective-permute-start(bf16[2,64,1024]{2,1,0:T(8,128)(2,1)} %collective-permute-done.18.refs_2_.rest_11_), channel_id=1, source_target_pairs={{0,16},{16,0},{1,17},{17,1},{2,18},{18,2},{3,19},{19,3},{4,20},{20... | collective-permute-start | bytes 786440 | tf_op jit(solution)/shard_map/ppermute | solution.py:232
  22.6 16.3 %copy-start.4 = (bf16[2,64,1024]{2,1,0:T(8,128)(2,1)}, bf16[2,64,1024]{2,1,0:T(8,128)(2,1)S(1)}, u32[]{:S(2)}) copy-start(bf16[2,64,1024]{2,1,0:T(8,128)(2,1)S(1)} %collective-permute-done.20.refs_4_.rest_13_) | copy-start | bytes 786436
  22.6 13.7 %collective-permute-start.25 = (bf16[2,64,1024]{2,1,0:T(8,128)(2,1)S(1)}, bf16[2,64,1024]{2,1,0:T(8,128)(2,1)S(1)}, u32[]{:S(2)}, u32[]{:S(2)}) collective-permute-start(bf16[2,64,1024]{2,1,0:T(8,128)(2,1)S(1)} %collective-permute-done.20.refs_4_.rest_13_), channel_id=1, source_target_pairs={{0,16},{16,0},{1,17},{17,1},{2,18},{18,2},{3,19},{19,3},{4,20},{20... | collective-permute-start | bytes 786440 | tf_op jit(solution)/shard_map/ppermute | solution.py:232
  38.9 17.1 %copy-start.1 = (bf16[3,2,64,1024]{3,2,1,0:T(8,128)(2,1)S(1)}, bf16[3,2,64,1024]{3,2,1,0:T(8,128)(2,1)}, u32[]{:S(2)}) copy-start(bf16[3,2,64,1024]{3,2,1,0:T(8,128)(2,1)} %rest_24_.3) | copy-start | bytes 2359300
  38.9 76.3 %collective-permute-start.26 = (bf16[10,2,64,1024]{3,2,1,0:T(8,128)(2,1)}, bf16[10,2,64,1024]{3,2,1,0:T(8,128)(2,1)}, u32[]{:S(2)}, u32[]{:S(2)}) collective-permute-start(bf16[10,2,64,1024]{3,2,1,0:T(8,128)(2,1)} %shard_map.42), channel_id=1, source_target_pairs={{0,1},{1,0},{2,3},{3,2},{4,5},{5,4},{6,7},{7,6},{8,9},{9,8},{10,11... | collective-permute-start | bytes 7864328 | tf_op jit(solution)/shard_map/ppermute | solution.py:229
  41.3 7.9 %collective-permute-start.27 = (bf16[2,64,1024]{2,1,0:T(8,128)(2,1)S(1)}, bf16[2,64,1024]{2,1,0:T(8,128)(2,1)}, u32[]{:S(2)}, u32[]{:S(2)}) collective-permute-start(bf16[2,64,1024]{2,1,0:T(8,128)(2,1)S(1)} %collective-permute-done.17.refs_1_.rest_10_), channel_id=1, source_target_pairs={{0,2},{1,3},{2,0},{3,1},{4,6},{5,7},{6,4},{7,5},{8,10},{9,11},{10,... | collective-permute-start | bytes 786440 | tf_op jit(solution)/shard_map/ppermute | solution.py:229
  41.5 13.3 %collective-permute-start.28 = (bf16[2,64,1024]{2,1,0:T(8,128)(2,1)}, bf16[2,64,1024]{2,1,0:T(8,128)(2,1)}, u32[]{:S(2)}, u32[]{:S(2)}) collective-permute-start(bf16[2,64,1024]{2,1,0:T(8,128)(2,1)} %collective-permute-done.18.refs_2_.rest_11_), channel_id=1, source_target_pairs={{0,2},{1,3},{2,0},{3,1},{4,6},{5,7},{6,4},{7,5},{8,10},{9,11},{10,... | collective-permute-start | bytes 786440 | tf_op jit(solution)/shard_map/ppermute | solution.py:229
  43.5 30.1 %collective-permute-start.8 = (bf16[2,8,32,1024]{3,2,1,0:T(8,128)(2,1)S(1)}, bf16[2,8,32,1024]{3,2,1,0:T(8,128)(2,1)S(1)}, u32[]{:S(2)}, u32[]{:S(2)}) collective-permute-start(bf16[2,8,32,1024]{3,2,1,0:T(8,128)(2,1)S(1)} %prep.1), channel_id=1, source_target_pairs={{0,1},{1,0},{2,3},{3,2},{4,5},{5,4},{6,7},{7,6},{8,9},{9,8},{10,11... | collective-permute-start | bytes 3145736 | tf_op jit(solution)/shard_map/ppermute | solution.py:229
  49.2 15.6 %collective-permute-start.29 = (bf16[2,64,1024]{2,1,0:T(8,128)(2,1)}, bf16[2,64,1024]{2,1,0:T(8,128)(2,1)S(1)}, u32[]{:S(2)}, u32[]{:S(2)}) collective-permute-start(bf16[2,64,1024]{2,1,0:T(8,128)(2,1)} %collective-permute-done.27.refs_0_.rest_19_), channel_id=1, source_target_pairs={{0,16},{16,0},{1,17},{17,1},{2,18},{18,2},{3,19},{19,3},{4,20},{20... | collective-permute-start | bytes 786440 | tf_op jit(solution)/shard_map/ppermute | solution.py:232
  54.8 10.0 %collective-permute-start.30 = (bf16[2,64,1024]{2,1,0:T(8,128)(2,1)}, bf16[2,64,1024]{2,1,0:T(8,128)(2,1)S(1)}, u32[]{:S(2)}, u32[]{:S(2)}) collective-permute-start(bf16[2,64,1024]{2,1,0:T(8,128)(2,1)} %collective-permute-done.28.refs_1_.rest_21_), channel_id=1, source_target_pairs={{0,16},{16,0},{1,17},{17,1},{2,18},{18,2},{3,19},{19,3},{4,20},{20... | collective-permute-start | bytes 786440 | tf_op jit(solution)/shard_map/ppermute | solution.py:232
  56.0 7.1 %collective-permute-start.1 = (bf16[1,64,1024]{2,1,0:T(8,128)(2,1)S(1)}, bf16[1,64,1024]{2,1,0:T(8,128)(2,1)S(1)}, u32[]{:S(2)}, u32[]{:S(2)}) collective-permute-start(bf16[1,64,1024]{2,1,0:T(8,128)(2,1)S(1)} %dynamic-slice_bitcast_fusion.2.refs_0_), channel_id=1, source_target_pairs={{0,12},{1,13},{2,14},{3,15},{4,8},{5,9},{6,10},{7,11},{8,4},{9,5},... | collective-permute-start | bytes 393224 | tf_op jit(solution)/shard_map/ppermute | solution.py:229
  63.1 23.2 %collective-permute-start.5 = (bf16[3,2,64,1024]{3,2,1,0:T(8,128)(2,1)S(1)}, bf16[3,2,64,1024]{3,2,1,0:T(8,128)(2,1)S(1)}, u32[]{:S(2)}, u32[]{:S(2)}) collective-permute-start(bf16[3,2,64,1024]{3,2,1,0:T(8,128)(2,1)S(1)} %copy-done.1), channel_id=1, source_target_pairs={{0,1},{1,0},{2,3},{3,2},{4,5},{5,4},{6,7},{7,6},{8,9},{9,8},{10,11... | collective-permute-start | bytes 2359304 | tf_op jit(solution)/shard_map/ppermute | solution.py:229
  64.8 5.1 %collective-permute-start = (bf16[1,64,1024]{2,1,0:T(8,128)(2,1)S(1)}, bf16[1,64,1024]{2,1,0:T(8,128)(2,1)S(1)}, u32[]{:S(2)}, u32[]{:S(2)}) collective-permute-start(bf16[1,64,1024]{2,1,0:T(8,128)(2,1)S(1)} %dynamic-slice_bitcast_fusion.2.refs_0_), channel_id=1, source_target_pairs={{0,4},{1,5},{2,6},{3,7},{4,0},{5,1},{6,2},{7,3},{8,12},{9,13},{10,... | collective-permute-start | bytes 393224 | tf_op jit(solution)/shard_map/ppermute | solution.py:229
  64.8 7.9 %collective-permute-start.2 = (bf16[1,64,1024]{2,1,0:T(8,128)(2,1)S(1)}, bf16[1,64,1024]{2,1,0:T(8,128)(2,1)S(1)}, u32[]{:S(2)}, u32[]{:S(2)}) collective-permute-start(bf16[1,64,1024]{2,1,0:T(8,128)(2,1)S(1)} %collective-permute-done.1.refs_2_.refs_1_.rest_2_), channel_id=1, source_target_pairs={{0,4},{1,5},{2,6},{3,7},{4,0},{5,1},{6,2},{7,3},{8,12},{9,13},{10,... | collective-permute-start | bytes 393224 | tf_op jit(solution)/shard_map/ppermute | solution.py:229
  69.8 45.2 %collective-permute-start.31 = (bf16[4,2,64,1024]{3,2,1,0:T(8,128)(2,1)S(1)}, bf16[4,2,64,1024]{3,2,1,0:T(8,128)(2,1)S(1)}, u32[]{:S(2)}, u32[]{:S(2)}) collective-permute-start(bf16[4,2,64,1024]{3,2,1,0:T(8,128)(2,1)S(1)} %shard_map.43), channel_id=1, source_target_pairs={{0,1},{1,0},{2,3},{3,2},{4,5},{5,4},{6,7},{7,6},{8,9},{9,8},{10,11... | collective-permute-start | bytes 3145736 | tf_op jit(solution)/shard_map/ppermute | solution.py:229
  73.4 30.8 %copy-start.16 = (s32[3,1024]{1,0:T(4,128)S(1)}, s32[3,1024]{1,0:T(4,128)}, u32[]{:S(2)}) copy-start(s32[3,1024]{1,0:T(4,128)} %param.5) | copy-start | bytes 36868
  73.4 12.7 %collective-permute-start.3 = (bf16[4,1,64,1024]{3,2,1,0:T(8,128)(2,1)S(1)}, bf16[4,1,64,1024]{3,2,1,0:T(8,128)(2,1)S(1)}, u32[]{:S(2)}, u32[]{:S(2)}) collective-permute-start(bf16[4,1,64,1024]{3,2,1,0:T(8,128)(2,1)S(1)} %shard_map.37), channel_id=1, source_target_pairs={{0,2},{1,3},{2,0},{3,1},{4,6},{5,7},{6,4},{7,5},{8,10},{9,11},{10,... | collective-permute-start | bytes 1572872 | tf_op jit(solution)/shard_map/ppermute | solution.py:229
  75.8 13.1 %collective-permute-start.9 = (bf16[2,2,16,1024]{3,2,1,0:T(8,128)(2,1)S(1)}, bf16[2,2,16,1024]{3,2,1,0:T(8,128)(2,1)S(1)}, u32[]{:S(2)}, u32[]{:S(2)}) collective-permute-start(bf16[2,2,16,1024]{3,2,1,0:T(8,128)(2,1)S(1)} %get-tuple-element.38), channel_id=1, source_target_pairs={{0,2},{1,3},{2,0},{3,1},{4,6},{5,7},{6,4},{7,5},{8,10},{9,11},{10,... | collective-permute-start | bytes 393224 | tf_op jit(solution)/shard_map/ppermute | solution.py:229
  86.1 5.4 %collective-permute-start.40 = (bf16[2,2,16,1024]{3,2,1,0:T(8,128)(2,1)S(1)}, bf16[2,2,16,1024]{3,2,1,0:T(8,128)(2,1)S(1)}, u32[]{:S(2)}, u32[]{:S(2)}) collective-permute-start(bf16[2,2,16,1024]{3,2,1,0:T(8,128)(2,1)S(1)} %get-tuple-element.54), channel_id=1, source_target_pairs={{0,2},{1,3},{2,0},{3,1},{4,6},{5,7},{6,4},{7,5},{8,10},{9,11},{10,... | collective-permute-start | bytes 393224 | tf_op jit(solution)/shard_map/ppermute | solution.py:229
  86.3 5.5 %collective-permute-start.41 = (bf16[2,2,16,1024]{3,2,1,0:T(8,128)(2,1)S(1)}, bf16[2,2,16,1024]{3,2,1,0:T(8,128)(2,1)S(1)}, u32[]{:S(2)}, u32[]{:S(2)}) collective-permute-start(bf16[2,2,16,1024]{3,2,1,0:T(8,128)(2,1)S(1)} %get-tuple-element.55), channel_id=1, source_target_pairs={{0,4},{1,5},{2,6},{3,7},{4,0},{5,1},{6,2},{7,3},{8,12},{9,13},{10,... | collective-permute-start | bytes 393224 | tf_op jit(solution)/shard_map/ppermute | solution.py:229
  88.9 5.0 %collective-permute-start.42 = (bf16[2,2,16,1024]{3,2,1,0:T(8,128)(2,1)S(1)}, bf16[2,2,16,1024]{3,2,1,0:T(8,128)(2,1)S(1)}, u32[]{:S(2)}, u32[]{:S(2)}) collective-permute-start(bf16[2,2,16,1024]{3,2,1,0:T(8,128)(2,1)S(1)} %get-tuple-element.56), channel_id=1, source_target_pairs={{0,6},{1,7},{2,4},{3,5},{4,2},{5,3},{6,0},{7,1},{8,14},{9,15},{10,... | collective-permute-start | bytes 393224 | tf_op jit(solution)/shard_map/ppermute | solution.py:229
  91.5 41.5 %collective-permute-start.6 = (bf16[7,1,64,1024]{3,2,1,0:T(8,128)(2,1)S(1)}, bf16[7,1,64,1024]{3,2,1,0:T(8,128)(2,1)S(1)}, u32[]{:S(2)}, u32[]{:S(2)}) collective-permute-start(bf16[7,1,64,1024]{3,2,1,0:T(8,128)(2,1)S(1)} %shard_map.38), channel_id=1, source_target_pairs={{0,16},{16,0},{1,17},{17,1},{2,18},{18,2},{3,19},{19,3},{4,20},{20... | collective-permute-start | bytes 2752520 | tf_op jit(solution)/shard_map/ppermute | solution.py:232
  91.8 5.8 %collective-permute-start.43 = (bf16[2,2,16,1024]{3,2,1,0:T(8,128)(2,1)S(1)}, bf16[2,2,16,1024]{3,2,1,0:T(8,128)(2,1)S(1)}, u32[]{:S(2)}, u32[]{:S(2)}) collective-permute-start(bf16[2,2,16,1024]{3,2,1,0:T(8,128)(2,1)S(1)} %get-tuple-element.57), channel_id=1, source_target_pairs={{0,8},{1,9},{2,10},{3,11},{4,12},{5,13},{6,14},{7,15},{8,0},{9,1},... | collective-permute-start | bytes 393224 | tf_op jit(solution)/shard_map/ppermute | solution.py:229
  93.8 8.9 %collective-permute-start.44 = (bf16[2,2,16,1024]{3,2,1,0:T(8,128)(2,1)S(1)}, bf16[2,2,16,1024]{3,2,1,0:T(8,128)(2,1)S(1)}, u32[]{:S(2)}, u32[]{:S(2)}) collective-permute-start(bf16[2,2,16,1024]{3,2,1,0:T(8,128)(2,1)S(1)} %get-tuple-element.58), channel_id=1, source_target_pairs={{0,10},{1,11},{2,8},{3,9},{4,14},{5,15},{6,12},{7,13},{8,2},{9,3},... | collective-permute-start | bytes 393224 | tf_op jit(solution)/shard_map/ppermute | solution.py:229
  97.5 11.0 %collective-permute-start.45 = (bf16[2,2,16,1024]{3,2,1,0:T(8,128)(2,1)S(1)}, bf16[2,2,16,1024]{3,2,1,0:T(8,128)(2,1)S(1)}, u32[]{:S(2)}, u32[]{:S(2)}) collective-permute-start(bf16[2,2,16,1024]{3,2,1,0:T(8,128)(2,1)S(1)} %get-tuple-element.59), channel_id=1, source_target_pairs={{0,12},{1,13},{2,14},{3,15},{4,8},{5,9},{6,10},{7,11},{8,4},{9,5},... | collective-permute-start | bytes 393224 | tf_op jit(solution)/shard_map/ppermute | solution.py:229
  102.7 11.9 %collective-permute-start.46 = (bf16[2,2,16,1024]{3,2,1,0:T(8,128)(2,1)S(1)}, bf16[2,2,16,1024]{3,2,1,0:T(8,128)(2,1)S(1)}, u32[]{:S(2)}, u32[]{:S(2)}) collective-permute-start(bf16[2,2,16,1024]{3,2,1,0:T(8,128)(2,1)S(1)} %get-tuple-element.60), channel_id=1, source_target_pairs={{0,14},{1,15},{2,12},{3,13},{4,10},{5,11},{6,8},{7,9},{8,6},{9,7},... | collective-permute-start | bytes 393224 | tf_op jit(solution)/shard_map/ppermute | solution.py:229
  104.2 13.9 %copy-start.3 = (bf16[2,64,1024]{2,1,0:T(8,128)(2,1)S(1)}, bf16[2,64,1024]{2,1,0:T(8,128)(2,1)}, u32[]{:S(2)}) copy-start(bf16[2,64,1024]{2,1,0:T(8,128)(2,1)} %copy-done.2) | copy-start | bytes 786436
  104.2 13.9 %copy-start.5 = (bf16[2,64,1024]{2,1,0:T(8,128)(2,1)S(1)}, bf16[2,64,1024]{2,1,0:T(8,128)(2,1)}, u32[]{:S(2)}) copy-start(bf16[2,64,1024]{2,1,0:T(8,128)(2,1)} %copy-done.4) | copy-start | bytes 786436
  104.2 13.9 %copy-start.7 = (bf16[2,64,1024]{2,1,0:T(8,128)(2,1)S(1)}, bf16[2,64,1024]{2,1,0:T(8,128)(2,1)}, u32[]{:S(2)}) copy-start(bf16[2,64,1024]{2,1,0:T(8,128)(2,1)} %copy-done.6) | copy-start | bytes 786436
  104.2 13.9 %copy-start.9 = (bf16[2,64,1024]{2,1,0:T(8,128)(2,1)S(1)}, bf16[2,64,1024]{2,1,0:T(8,128)(2,1)}, u32[]{:S(2)}) copy-start(bf16[2,64,1024]{2,1,0:T(8,128)(2,1)} %copy-done.8) | copy-start | bytes 786436
  108.5 18.7 %collective-permute-start.10 = (bf16[2,2,16,1024]{3,2,1,0:T(8,128)(2,1)S(1)}, bf16[2,2,16,1024]{3,2,1,0:T(8,128)(2,1)S(1)}, u32[]{:S(2)}, u32[]{:S(2)}) collective-permute-start(bf16[2,2,16,1024]{3,2,1,0:T(8,128)(2,1)S(1)} %get-tuple-element.39), channel_id=1, source_target_pairs={{0,4},{1,5},{2,6},{3,7},{4,0},{5,1},{6,2},{7,3},{8,12},{9,13},{10,... | collective-permute-start | bytes 393224 | tf_op jit(solution)/shard_map/ppermute | solution.py:229
  114.6 12.8 %collective-permute-start.11 = (bf16[2,2,16,1024]{3,2,1,0:T(8,128)(2,1)S(1)}, bf16[2,2,16,1024]{3,2,1,0:T(8,128)(2,1)S(1)}, u32[]{:S(2)}, u32[]{:S(2)}) collective-permute-start(bf16[2,2,16,1024]{3,2,1,0:T(8,128)(2,1)S(1)} %get-tuple-element.40), channel_id=1, source_target_pairs={{0,6},{1,7},{2,4},{3,5},{4,2},{5,3},{6,0},{7,1},{8,14},{9,15},{10,... | collective-permute-start | bytes 393224 | tf_op jit(solution)/shard_map/ppermute | solution.py:229
  115.0 13.9 %collective-permute-start.12 = (bf16[2,2,16,1024]{3,2,1,0:T(8,128)(2,1)S(1)}, bf16[2,2,16,1024]{3,2,1,0:T(8,128)(2,1)S(1)}, u32[]{:S(2)}, u32[]{:S(2)}) collective-permute-start(bf16[2,2,16,1024]{3,2,1,0:T(8,128)(2,1)S(1)} %get-tuple-element.41), channel_id=1, source_target_pairs={{0,8},{1,9},{2,10},{3,11},{4,12},{5,13},{6,14},{7,15},{8,0},{9,1},... | collective-permute-start | bytes 393224 | tf_op jit(solution)/shard_map/ppermute | solution.py:229
  115.2 14.8 %collective-permute-start.13 = (bf16[2,2,16,1024]{3,2,1,0:T(8,128)(2,1)S(1)}, bf16[2,2,16,1024]{3,2,1,0:T(8,128)(2,1)S(1)}, u32[]{:S(2)}, u32[]{:S(2)}) collective-permute-start(bf16[2,2,16,1024]{3,2,1,0:T(8,128)(2,1)S(1)} %get-tuple-element.42), channel_id=1, source_target_pairs={{0,10},{1,11},{2,8},{3,9},{4,14},{5,15},{6,12},{7,13},{8,2},{9,3},... | collective-permute-start | bytes 393224 | tf_op jit(solution)/shard_map/ppermute | solution.py:229
  127.2 7.5 %collective-permute-start.14 = (bf16[2,2,16,1024]{3,2,1,0:T(8,128)(2,1)S(1)}, bf16[2,2,16,1024]{3,2,1,0:T(8,128)(2,1)S(1)}, u32[]{:S(2)}, u32[]{:S(2)}) collective-permute-start(bf16[2,2,16,1024]{3,2,1,0:T(8,128)(2,1)S(1)} %get-tuple-element.43), channel_id=1, source_target_pairs={{0,12},{1,13},{2,14},{3,15},{4,8},{5,9},{6,10},{7,11},{8,4},{9,5},... | collective-permute-start | bytes 393224 | tf_op jit(solution)/shard_map/ppermute | solution.py:229
  127.4 13.1 %collective-permute-start.15 = (bf16[2,2,16,1024]{3,2,1,0:T(8,128)(2,1)S(1)}, bf16[2,2,16,1024]{3,2,1,0:T(8,128)(2,1)S(1)}, u32[]{:S(2)}, u32[]{:S(2)}) collective-permute-start(bf16[2,2,16,1024]{3,2,1,0:T(8,128)(2,1)S(1)} %get-tuple-element.44), channel_id=1, source_target_pairs={{0,14},{1,15},{2,12},{3,13},{4,10},{5,11},{6,8},{7,9},{8,6},{9,7},... | collective-permute-start | bytes 393224 | tf_op jit(solution)/shard_map/ppermute | solution.py:229
  129.0 13.4 %collective-permute-start.47 = (bf16[2,2,16,1024]{3,2,1,0:T(8,128)(2,1)S(1)}, bf16[2,2,16,1024]{3,2,1,0:T(8,128)(2,1)S(1)}, u32[]{:S(2)}, u32[]{:S(2)}) collective-permute-start(bf16[2,2,16,1024]{3,2,1,0:T(8,128)(2,1)S(1)} %get-tuple-element.62), channel_id=1, source_target_pairs={{0,2},{1,3},{2,0},{3,1},{4,6},{5,7},{6,4},{7,5},{8,10},{9,11},{10,... | collective-permute-start | bytes 393224 | tf_op jit(solution)/shard_map/ppermute | solution.py:229
  130.0 13.6 %collective-permute-start.48 = (bf16[2,2,16,1024]{3,2,1,0:T(8,128)(2,1)S(1)}, bf16[2,2,16,1024]{3,2,1,0:T(8,128)(2,1)S(1)}, u32[]{:S(2)}, u32[]{:S(2)}) collective-permute-start(bf16[2,2,16,1024]{3,2,1,0:T(8,128)(2,1)S(1)} %get-tuple-element.63), channel_id=1, source_target_pairs={{0,4},{1,5},{2,6},{3,7},{4,0},{5,1},{6,2},{7,3},{8,12},{9,13},{10,... | collective-permute-start | bytes 393224 | tf_op jit(solution)/shard_map/ppermute | solution.py:229
  133.0 12.0 %collective-permute-start.49 = (bf16[2,2,16,1024]{3,2,1,0:T(8,128)(2,1)S(1)}, bf16[2,2,16,1024]{3,2,1,0:T(8,128)(2,1)S(1)}, u32[]{:S(2)}, u32[]{:S(2)}) collective-permute-start(bf16[2,2,16,1024]{3,2,1,0:T(8,128)(2,1)S(1)} %get-tuple-element.64), channel_id=1, source_target_pairs={{0,6},{1,7},{2,4},{3,5},{4,2},{5,3},{6,0},{7,1},{8,14},{9,15},{10,... | collective-permute-start | bytes 393224 | tf_op jit(solution)/shard_map/ppermute | solution.py:229
  134.8 60.9 %collective-permute-start.4 = (bf16[7,1,64,1024]{3,2,1,0:T(8,128)(2,1)S(1)}, bf16[7,1,64,1024]{3,2,1,0:T(8,128)(2,1)S(1)}, u32[]{:S(2)}, u32[]{:S(2)}) collective-permute-start(bf16[7,1,64,1024]{3,2,1,0:T(8,128)(2,1)S(1)} %shard_map.38), channel_id=1, source_target_pairs={{0,1},{1,0},{2,3},{3,2},{4,5},{5,4},{6,7},{7,6},{8,9},{9,8},{10,11... | collective-permute-start | bytes 2752520 | tf_op jit(solution)/shard_map/ppermute | solution.py:229
  140.5 58.1 %collective-permute-start.7 = (bf16[7,1,64,1024]{3,2,1,0:T(8,128)(2,1)S(1)}, bf16[7,1,64,1024]{3,2,1,0:T(8,128)(2,1)S(1)}, u32[]{:S(2)}, u32[]{:S(2)}) collective-permute-start(bf16[7,1,64,1024]{3,2,1,0:T(8,128)(2,1)S(1)} %shard_map.40), channel_id=1, source_target_pairs={{0,1},{1,0},{2,3},{3,2},{4,5},{5,4},{6,7},{7,6},{8,9},{9,8},{10,11... | collective-permute-start | bytes 2752520 | tf_op jit(solution)/shard_map/ppermute | solution.py:229
  142.4 12.2 %collective-permute-start.50 = (bf16[2,2,16,1024]{3,2,1,0:T(8,128)(2,1)S(1)}, bf16[2,2,16,1024]{3,2,1,0:T(8,128)(2,1)S(1)}, u32[]{:S(2)}, u32[]{:S(2)}) collective-permute-start(bf16[2,2,16,1024]{3,2,1,0:T(8,128)(2,1)S(1)} %get-tuple-element.65), channel_id=1, source_target_pairs={{0,8},{1,9},{2,10},{3,11},{4,12},{5,13},{6,14},{7,15},{8,0},{9,1},... | collective-permute-start | bytes 393224 | tf_op jit(solution)/shard_map/ppermute | solution.py:229
  143.5 13.4 %collective-permute-start.51 = (bf16[2,2,16,1024]{3,2,1,0:T(8,128)(2,1)S(1)}, bf16[2,2,16,1024]{3,2,1,0:T(8,128)(2,1)S(1)}, u32[]{:S(2)}, u32[]{:S(2)}) collective-permute-start(bf16[2,2,16,1024]{3,2,1,0:T(8,128)(2,1)S(1)} %get-tuple-element.66), channel_id=1, source_target_pairs={{0,10},{1,11},{2,8},{3,9},{4,14},{5,15},{6,12},{7,13},{8,2},{9,3},... | collective-permute-start | bytes 393224 | tf_op jit(solution)/shard_map/ppermute | solution.py:229
  145.0 14.8 %collective-permute-start.52 = (bf16[2,2,16,1024]{3,2,1,0:T(8,128)(2,1)S(1)}, bf16[2,2,16,1024]{3,2,1,0:T(8,128)(2,1)S(1)}, u32[]{:S(2)}, u32[]{:S(2)}) collective-permute-start(bf16[2,2,16,1024]{3,2,1,0:T(8,128)(2,1)S(1)} %get-tuple-element.67), channel_id=1, source_target_pairs={{0,12},{1,13},{2,14},{3,15},{4,8},{5,9},{6,10},{7,11},{8,4},{9,5},... | collective-permute-start | bytes 393224 | tf_op jit(solution)/shard_map/ppermute | solution.py:229
  154.6 12.4 %collective-permute-start.53 = (bf16[2,2,16,1024]{3,2,1,0:T(8,128)(2,1)S(1)}, bf16[2,2,16,1024]{3,2,1,0:T(8,128)(2,1)S(1)}, u32[]{:S(2)}, u32[]{:S(2)}) collective-permute-start(bf16[2,2,16,1024]{3,2,1,0:T(8,128)(2,1)S(1)} %get-tuple-element.68), channel_id=1, source_target_pairs={{0,14},{1,15},{2,12},{3,13},{4,10},{5,11},{6,8},{7,9},{8,6},{9,7},... | collective-permute-start | bytes 393224 | tf_op jit(solution)/shard_map/ppermute | solution.py:229
  157.0 10.0 %collective-permute-start.32 = (bf16[2,2,16,1024]{3,2,1,0:T(8,128)(2,1)S(1)}, bf16[2,2,16,1024]{3,2,1,0:T(8,128)(2,1)S(1)}, u32[]{:S(2)}, u32[]{:S(2)}) collective-permute-start(bf16[2,2,16,1024]{3,2,1,0:T(8,128)(2,1)S(1)} %get-tuple-element.46), channel_id=1, source_target_pairs={{0,2},{1,3},{2,0},{3,1},{4,6},{5,7},{6,4},{7,5},{8,10},{9,11},{10,... | collective-permute-start | bytes 393224 | tf_op jit(solution)/shard_map/ppermute | solution.py:229
  159.8 9.9 %collective-permute-start.33 = (bf16[2,2,16,1024]{3,2,1,0:T(8,128)(2,1)S(1)}, bf16[2,2,16,1024]{3,2,1,0:T(8,128)(2,1)S(1)}, u32[]{:S(2)}, u32[]{:S(2)}) collective-permute-start(bf16[2,2,16,1024]{3,2,1,0:T(8,128)(2,1)S(1)} %get-tuple-element.47), channel_id=1, source_target_pairs={{0,4},{1,5},{2,6},{3,7},{4,0},{5,1},{6,2},{7,3},{8,12},{9,13},{10,... | collective-permute-start | bytes 393224 | tf_op jit(solution)/shard_map/ppermute | solution.py:229
  167.0 5.2 %collective-permute-start.34 = (bf16[2,2,16,1024]{3,2,1,0:T(8,128)(2,1)S(1)}, bf16[2,2,16,1024]{3,2,1,0:T(8,128)(2,1)S(1)}, u32[]{:S(2)}, u32[]{:S(2)}) collective-permute-start(bf16[2,2,16,1024]{3,2,1,0:T(8,128)(2,1)S(1)} %get-tuple-element.48), channel_id=1, source_target_pairs={{0,6},{1,7},{2,4},{3,5},{4,2},{5,3},{6,0},{7,1},{8,14},{9,15},{10,... | collective-permute-start | bytes 393224 | tf_op jit(solution)/shard_map/ppermute | solution.py:229
  167.0 8.7 %collective-permute-start.35 = (bf16[2,2,16,1024]{3,2,1,0:T(8,128)(2,1)S(1)}, bf16[2,2,16,1024]{3,2,1,0:T(8,128)(2,1)S(1)}, u32[]{:S(2)}, u32[]{:S(2)}) collective-permute-start(bf16[2,2,16,1024]{3,2,1,0:T(8,128)(2,1)S(1)} %get-tuple-element.49), channel_id=1, source_target_pairs={{0,8},{1,9},{2,10},{3,11},{4,12},{5,13},{6,14},{7,15},{8,0},{9,1},... | collective-permute-start | bytes 393224 | tf_op jit(solution)/shard_map/ppermute | solution.py:229
  169.7 13.7 %collective-permute-start.36 = (bf16[2,2,16,1024]{3,2,1,0:T(8,128)(2,1)S(1)}, bf16[2,2,16,1024]{3,2,1,0:T(8,128)(2,1)S(1)}, u32[]{:S(2)}, u32[]{:S(2)}) collective-permute-start(bf16[2,2,16,1024]{3,2,1,0:T(8,128)(2,1)S(1)} %get-tuple-element.50), channel_id=1, source_target_pairs={{0,10},{1,11},{2,8},{3,9},{4,14},{5,15},{6,12},{7,13},{8,2},{9,3},... | collective-permute-start | bytes 393224 | tf_op jit(solution)/shard_map/ppermute | solution.py:229
  172.2 14.2 %collective-permute-start.37 = (bf16[2,2,16,1024]{3,2,1,0:T(8,128)(2,1)S(1)}, bf16[2,2,16,1024]{3,2,1,0:T(8,128)(2,1)S(1)}, u32[]{:S(2)}, u32[]{:S(2)}) collective-permute-start(bf16[2,2,16,1024]{3,2,1,0:T(8,128)(2,1)S(1)} %get-tuple-element.51), channel_id=1, source_target_pairs={{0,12},{1,13},{2,14},{3,15},{4,8},{5,9},{6,10},{7,11},{8,4},{9,5},... | collective-permute-start | bytes 393224 | tf_op jit(solution)/shard_map/ppermute | solution.py:229
  175.7 15.1 %collective-permute-start.38 = (bf16[2,2,16,1024]{3,2,1,0:T(8,128)(2,1)S(1)}, bf16[2,2,16,1024]{3,2,1,0:T(8,128)(2,1)S(1)}, u32[]{:S(2)}, u32[]{:S(2)}) collective-permute-start(bf16[2,2,16,1024]{3,2,1,0:T(8,128)(2,1)S(1)} %get-tuple-element.52), channel_id=1, source_target_pairs={{0,14},{1,15},{2,12},{3,13},{4,10},{5,11},{6,8},{7,9},{8,6},{9,7},... | collective-permute-start | bytes 393224 | tf_op jit(solution)/shard_map/ppermute | solution.py:229
  183.4 18.1 %collective-permute-start.54 = (bf16[8,2,16,1024]{3,2,1,0:T(8,128)(2,1)S(1)}, bf16[8,2,16,1024]{3,2,1,0:T(8,128)(2,1)S(1)}, u32[]{:S(2)}, u32[]{:S(2)}) collective-permute-start(bf16[8,2,16,1024]{3,2,1,0:T(8,128)(2,1)S(1)} %shard_map.47), channel_id=1, source_target_pairs={{0,1},{1,0},{2,3},{3,2},{4,5},{5,4},{6,7},{7,6},{8,9},{9,8},{10,11... | collective-permute-start | bytes 1572872 | tf_op jit(solution)/shard_map/ppermute | solution.py:229
  191.7 13.7 %collective-permute-start.39 = (bf16[8,2,16,1024]{3,2,1,0:T(8,128)(2,1)S(1)}, bf16[8,2,16,1024]{3,2,1,0:T(8,128)(2,1)S(1)}, u32[]{:S(2)}, u32[]{:S(2)}) collective-permute-start(bf16[8,2,16,1024]{3,2,1,0:T(8,128)(2,1)S(1)} %shard_map.45), channel_id=1, source_target_pairs={{0,1},{1,0},{2,3},{3,2},{4,5},{5,4},{6,7},{7,6},{8,9},{9,8},{10,11... | collective-permute-start | bytes 1572872 | tf_op jit(solution)/shard_map/ppermute | solution.py:229
  (8 other events, 86.8 us)
